TPU v7x, 32 devices: a whole 2x2x4 slice. The times are simulated.
32 devices in a mesh: rows: 8 (over z, y), grp: 4 (over x, core).
Axes of the slice: x: 2, y: 2, z: 4, core: 2. Of those that a mesh axis runs over, the one named last changes fastest.
Arguments:
- modes: float32 [393216, 256], P(('rows', 'grp')), may hold values from -6 to 6
- points: int32 [196], replicated, may hold values from 0 to 393215, as said below
Outputs:
- residual: float32 [393216, 128], P(('rows', 'grp'))
- norms: float32 [4, 128], replicated
Inputs may be any that keep to these rules, and one draw needn't show every extreme that they name: `points`: distinct row indices of the mode matrix.
All inputs are finite; a program needn't handle non-finite values.
Results may differ from a plain program's by a relative error of at most 0.00029.
Values sent between devices are 32-bit elements; how exact they have to be, the bound alone decides.
A program may use at most 128 MiB of HBM per device.

v0:
```python
import functools

import jax
import jax.numpy as jnp
from jax import lax
from jax.experimental import pallas as pl
from jax.experimental.pallas import tpu as pltpu
from jax.sharding import PartitionSpec as P

PRIOR = 192
BLOCK = 8
HOOK_AT = 80
EARLY, FIRST = 2, 6
HIGH = lax.Precision.HIGHEST
MESH = pl.DeviceIdType.MESH


def dot(a, b, dims=((1,), (0,))):
    return lax.dot_general(a, b, (dims, ((), ())), precision=HIGH, preferred_element_type=jnp.float32)


def flat_index(axes):
    (first, _), (second, width) = axes
    return lax.axis_index(first) * width + lax.axis_index(second)


def coords(axes, flat):
    width = axes[1][1]
    return (flat // width, lax.rem(flat, width))


def pick_kernel(axes, n, points_ref, modes_ref, out_ref, picked, sem):
    rows_dev, cols = modes_ref.shape
    npts = points_ref.shape[0]
    split = cols // 2
    base = flat_index(axes) * rows_dev
    picked[...] = jnp.zeros_like(picked)

    def row_copy(i):
        local = points_ref[i] - base
        owned = (local >= 0) & (local < rows_dev)
        safe = jnp.clip(local, 0, rows_dev - 1)
        return owned, pltpu.make_async_copy(
            modes_ref.at[pl.ds(safe, 1), :], picked.at[pl.ds(i, 1), :], sem
        )

    def issue(i, count):
        owned, copy = row_copy(i)

        @pl.when(owned)
        def _():
            copy.start()

        return count

    def drain(i, count):
        owned, copy = row_copy(i)

        @pl.when(owned)
        def _():
            copy.wait()

        return count

    lax.fori_loop(0, npts, issue, 0, unroll=4)
    lax.fori_loop(0, npts, drain, 0, unroll=4)
    block = picked[...]
    index = lax.broadcasted_iota(jnp.int32, block.shape, 0)
    chosen = jnp.where(index <= PRIOR, block, 0.0)
    both = dot(chosen[:, :split], chosen, ((0,), (0,)))
    rp = 2 * split // n
    for i in range(n):
        row, col = (i * rp) % split, (i * rp) // split * split
        out_ref[i, 0:rp, :] = both[row : row + rp, col : col + split]
    fresh = npts - PRIOR - 1
    out_ref[:, rp : rp + 1, :] = jnp.zeros((n, 1, split), jnp.float32)
    for i in range(fresh):
        for half in range(2):
            at = PRIOR + 1 + i
            out_ref[2 * i + half, rp : rp + 1, :] = picked[at : at + 1, half * split : (half + 1) * split]


def barrier_all(axes, n, me):
    barrier = pltpu.get_barrier_semaphore()

    def greet(off, carry):
        peer = lax.rem(me + off, n)
        pl.semaphore_signal(barrier, inc=1, device_id=coords(axes, peer), device_id_type=MESH)
        return carry

    lax.fori_loop(1, n, greet, 0)
    pl.semaphore_wait(barrier, n - 1)


def small_inverse(e):
    size = len(e)
    e = [list(line) for line in e]
    for p in range(size):
        inv = 1.0 / e[p][p]
        line = [e[p][j] * inv for j in range(size)]
        line[p] = -inv
        for i in range(size):
            for j in range(i, size):
                if i == p or j == p:
                    continue
                e[i][j] = e[i][j] - e[p][i] * line[j]
                e[j][i] = e[i][j]
        for j in range(size):
            e[p][j] = line[j]
            e[j][p] = line[j]
    return [[-value for value in line] for line in e]


def sweep_inverse(gram, hook, width=BLOCK):
    size = gram.shape[0]
    shape = (8, size)
    tiles = [gram[8 * t : 8 * t + 8, :] for t in range(size // 8)]
    lane = lax.broadcasted_iota(jnp.int32, shape, 1)
    sub = lax.broadcasted_iota(jnp.int32, shape, 0)
    for k in range(0, size, width):
        if k == HOOK_AT:
            hook()
        t, s = k // 8, k % 8
        inside = (lane >= k) & (lane < k + width)
        own = [jnp.broadcast_to(tiles[t][:, k + q : k + q + 1], shape) for q in range(width)]
        entry = [[None] * width for _ in range(width)]
        for p in range(width):
            for q in range(p, width):
                entry[p][q] = jnp.broadcast_to(own[q][s + p : s + p + 1, :], shape)
                entry[q][p] = entry[p][q]
        small = small_inverse(entry)
        rows = []
        for q in range(width):
            row = jnp.broadcast_to(tiles[t][s + q : s + q + 1, :], shape)
            rows.append(jnp.where(inside, jnp.where(lane == k + q, -1.0, 0.0), row))
        scaled = []
        for p in range(width):
            line = small[p][0] * rows[0]
            for q in range(1, width):
                line = line + small[p][q] * rows[q]
            scaled.append(line)
        fresh = []
        for r in range(size // 8):
            value = jnp.where(inside, 0.0, tiles[r])
            for p in range(width):
                col = own[p] if r == t else jnp.broadcast_to(tiles[r][:, k + p : k + p + 1], shape)
                value = value - col * scaled[p]
            fresh.append(value)
        for p in range(width):
            fresh[t] = jnp.where(sub == s + p, scaled[p], fresh[t])
        tiles = fresh
    return -jnp.concatenate(tiles, axis=0)


def solve_kernel(
    axes, n, part_ref, modes_ref, wide_ref, norm_ref,
    landed, mine, full, part2, landed2, mine2, full2, square, held, acc, squares,
    send1, recv1, send2, recv2, local,
):
    me = flat_index(axes)
    rp = part_ref.shape[1] - 1
    split = part_ref.shape[2]
    steps = norm_ref.shape[0]
    chunks, rows = held.shape[0], held.shape[1]
    total_rows = chunks * rows * n

    def loop(body, first=1, last=n):
        def step(off, carry):
            body(off)
            return carry

        lax.fori_loop(first, last, step, 0)

    def fetch(c):
        return pltpu.make_async_copy(
            modes_ref.at[pl.ds(c * rows, rows), :], held.at[c], local.at[c]
        )

    loop(lambda c: fetch(c).start(), 0, chunks)
    barrier = pltpu.get_barrier_semaphore()

    def greet(off):
        peer = lax.rem(me + off, n)
        pl.semaphore_signal(barrier, inc=1, device_id=coords(axes, peer), device_id_type=MESH)

    loop(greet)
    acc[...] = jnp.zeros_like(acc)
    squares[...] = jnp.zeros_like(squares)

    def grams(c):
        fetch(c).wait()
        acc[...] += dot(held[c, :, :split], held[c], ((0,), (0,)))
        rest = held[c, :, split:]
        squares[...] += jnp.sum((rest * rest).reshape(-1, 8, split), axis=0)

    def scatter(src, dst, off):
        peer = lax.rem(me + off, n)
        return pltpu.make_async_remote_copy(
            src_ref=src.at[peer],
            dst_ref=dst.at[off],
            send_sem=send1.at[off],
            recv_sem=recv1.at[off],
            device_id=coords(axes, peer),
            device_id_type=MESH,
        )

    def spread(src, dst, off):
        peer = lax.rem(me + off, n)
        return pltpu.make_async_remote_copy(
            src_ref=src,
            dst_ref=dst.at[me],
            send_sem=send2.at[off],
            recv_sem=recv2.at[off],
            device_id=coords(axes, peer),
            device_id_type=MESH,
        )

    def gathered(src, dst, off):
        owner = lax.rem(me - off + n, n)
        return pltpu.make_async_remote_copy(
            src_ref=src,
            dst_ref=dst.at[owner],
            send_sem=send2.at[off],
            recv_sem=recv2.at[off],
            device_id=coords(axes, owner),
            device_id_type=MESH,
        )

    def reduced(src, got, own, whole):
        loop(lambda off: scatter(src, got, off).wait_recv())
        total = src[me]
        for off in range(1, n):
            total = total + got[off]
        own[...] = total
        whole[me] = total
        loop(lambda off: scatter(src, got, off).wait_send())
        loop(lambda off: spread(own, whole, off).start())

    def finish(own, whole):
        loop(lambda off: gathered(own, whole, off).wait_recv())
        loop(lambda off: spread(own, whole, off).wait_send())
        for i in range(n):
            square[i * rp : (i + 1) * rp, :] = whole[i, 0:rp, :]
        return square[0:split, :], square[split : 2 * split, :]

    early, first = min(EARLY, chunks), min(FIRST, chunks)
    loop(grams, 0, early)
    pl.semaphore_wait(barrier, n - 1)
    loop(lambda off: scatter(part_ref, landed, off).start())
    loop(grams, early, first)
    reduced(part_ref, landed, mine, full)
    loop(grams, first, chunks)
    part2[...] = jnp.zeros_like(part2)
    for i in range(n):
        row, col = (i * rp) % split, (i * rp) // split * split
        part2[i, 0:rp, :] = acc[row : row + rp, col : col + split]
    part2[0, rp : rp + 1, :] = jnp.sum(squares[...], axis=0, keepdims=True)
    gram, cross = finish(mine, full)
    loop(lambda off: scatter(part2, landed2, off).start())
    inverse = sweep_inverse(gram, lambda: reduced(part2, landed2, mine2, full2))
    coef = dot(inverse, cross)
    coef = coef + dot(inverse, cross - dot(gram, coef))
    left = [full[2 * i, rp : rp + 1, :] for i in range(3)]
    right = [full[2 * i + 1, rp : rp + 1, :] for i in range(3)]
    pad = jnp.zeros((5, split), jnp.float32)
    lefts = jnp.concatenate(left + [pad], axis=0)
    gains = dot(lefts, inverse)
    errors = dot(lefts, coef)
    ks, ss, ds = [], [], []
    kept = [coef]
    pad7 = jnp.zeros((7, split), jnp.float32)
    for j in range(3):
        k = gains[j : j + 1, :]
        d = right[j] - errors[j : j + 1, :]
        for k0, s0, d0 in zip(ks, ss, ds):
            along = jnp.sum(k0 * left[j], axis=1, keepdims=True)
            k = k - k0 * (along / s0)
            d = d - along * d0
        s = 1.0 + jnp.sum(k * left[j], axis=1, keepdims=True)
        d = d / s
        ks.append(k)
        ss.append(s)
        ds.append(d)
        turn = dot(jnp.concatenate([k, pad7], axis=0), jnp.concatenate([d, pad7], axis=0), ((0,), (0,)))
        kept.append(kept[-1] + turn)
    c_hi, c_lo = halves(kept[-1])
    wide_ref[0:split, 0:split] = c_hi
    wide_ref[split:, 0:split] = c_hi
    wide_ref[0:split, split : 2 * split] = c_lo
    wide_ref[split:, split : 2 * split] = jnp.zeros((split, split), jnp.bfloat16)
    ftf, ftr = finish(mine2, full2)
    sq = full2[0, rp : rp + 1, :]
    curved = dot(ftf, jnp.concatenate(kept, axis=1))
    for j in range(steps):
        bent = kept[j] * (curved[:, j * split : (j + 1) * split] - 2.0 * ftr)
        norm_ref[j : j + 1, :] = (sq + jnp.sum(bent, axis=0, keepdims=True)) / total_rows


def halves(value):
    hi = value.astype(jnp.bfloat16)
    return hi, (value - hi.astype(jnp.float32)).astype(jnp.bfloat16)


def residual_kernel(modes_ref, wide_ref, res_ref, held, made_buf, read, wrote):
    chunks, rows, split = made_buf.shape
    piece = 256 if rows % 256 == 0 else rows

    def fetch(c):
        return pltpu.make_async_copy(modes_ref.at[pl.ds(c * rows, rows), :], held.at[c], read.at[c])

    def flush(c):
        return pltpu.make_async_copy(made_buf.at[c], res_ref.at[pl.ds(c * rows, rows), :], wrote.at[c])

    for c in range(chunks):
        fetch(c).start()
    wide = wide_ref[...]
    for c in range(chunks):
        fetch(c).wait()
        for at in range(0, rows, piece):
            hi, lo = halves(held[c, at : at + piece, :split])
            pair = jnp.concatenate([hi, lo], axis=1)
            made = jnp.dot(pair, wide, preferred_element_type=jnp.float32)
            made_buf[c, at : at + piece, :] = held[c, at : at + piece, split:] - (made[:, :split] + made[:, split:])
        flush(c).start()
    for c in range(chunks):
        flush(c).wait()


def on_device(axes, modes, points):
    n = axes[0][1] * axes[1][1]
    rows_dev, cols = modes.shape
    split = cols // 2
    rp = 2 * split // n
    npts = points.shape[0]
    steps = npts - PRIOR
    padded = -(-npts // 8) * 8
    f32 = jnp.float32
    vmem = pl.BlockSpec(memory_space=pltpu.VMEM)
    part = pl.pallas_call(
        functools.partial(pick_kernel, axes, n),
        out_shape=jax.ShapeDtypeStruct((n, rp + 1, split), f32),
        in_specs=[pl.BlockSpec(memory_space=pltpu.SMEM), pl.BlockSpec(memory_space=pl.ANY)],
        out_specs=vmem,
        scratch_shapes=[pltpu.VMEM((padded, cols), f32), pltpu.SemaphoreType.DMA],
        name="pick",
    )(points, modes)
    chunks = 12 if rows_dev % 96 == 0 else 1
    chunk_shape = pltpu.VMEM((n, rp + 1, split), f32)
    own_shape = pltpu.VMEM((rp + 1, split), f32)
    wide, norms = pl.pallas_call(
        functools.partial(solve_kernel, axes, n),
        out_shape=[
            jax.ShapeDtypeStruct((2 * split, 2 * split), jnp.bfloat16),
            jax.ShapeDtypeStruct((steps, split), f32),
        ],
        in_specs=[vmem, pl.BlockSpec(memory_space=pl.ANY)],
        out_specs=[vmem, vmem],
        scratch_shapes=[
            chunk_shape,
            own_shape,
            chunk_shape,
            chunk_shape,
            chunk_shape,
            own_shape,
            chunk_shape,
            pltpu.VMEM((2 * split, split), f32),
            pltpu.VMEM((chunks, rows_dev // chunks, cols), f32),
            pltpu.VMEM((split, cols), f32),
            pltpu.VMEM((8, split), f32),
        ]
        + [pltpu.SemaphoreType.DMA((n,))] * 4
        + [pltpu.SemaphoreType.DMA((chunks,))],
        compiler_params=pltpu.CompilerParams(collective_id=0, has_side_effects=True),
        name="solve",
    )(part, modes)
    any_space = pl.BlockSpec(memory_space=pl.ANY)
    residual = pl.pallas_call(
        residual_kernel,
        out_shape=jax.ShapeDtypeStruct((rows_dev, split), f32),
        in_specs=[any_space, vmem],
        out_specs=any_space,
        scratch_shapes=[
            pltpu.VMEM((chunks, rows_dev // chunks, cols), f32),
            pltpu.VMEM((chunks, rows_dev // chunks, split), f32),
            pltpu.SemaphoreType.DMA((chunks,)),
            pltpu.SemaphoreType.DMA((chunks,)),
        ],
        name="residual",
    )(modes, wide)
    return residual, norms


def solution(mesh):
    axes = tuple((name, mesh.shape[name]) for name in ("rows", "grp"))
    return jax.shard_map(
        functools.partial(on_device, axes),
        mesh=mesh,
        in_specs=(P(("rows", "grp"), None), P()),
        out_specs=(P(("rows", "grp"), None), P()),
        check_vma=False,
    )
```

profile of v0, /device:TPU:0, one launch (start us, length us, event | category | flops | bytes accessed | tf_op | source)
XLA Modules:
  0.0 47.7 jit_solution(6625260104045066040)
XLA Ops:
  0.6 4.6 %pick.1.part_ref = f32[32,9,128]{2,1,0:T(8,128)} custom-call(s32[196]{0:T(256)} %points_ref.1, f32[12288,256]{1,0:T(8,128)} %modes_ref.5), custom_call_target="tpu_custom_call" | custom-call | tf_op jit(solution)/shard_map/pick/pallas_call | solution.py:339
  5.3 33.3 %solve.1 = (bf16[256,256]{1,0:T(8,128)(2,1)}, f32[4,128]{1,0:T(4,128)}) custom-call(f32[32,9,128]{2,1,0:T(8,128)} %pick.1.part_ref, f32[12288,256]{1,0:T(8,128)} %modes_ref.5), custom_call_target="tpu_custom_call" | custom-call | tf_op jit(solution)/shard_map/solve/pallas_call | solution.py:350
  38.6 0.0 copy-start
  38.6 8.5 %residual.1 = f32[12288,128]{1,0:T(8,128)} custom-call(f32[12288,256]{1,0:T(8,128)} %modes_ref.5, bf16[256,256]{1,0:T(8,128)(2,1)} %get-tuple-element.4.wide_ref), custom_call_target="tpu_custom_call" | custom-call | tf_op jit(solution)/shard_map/residual/pallas_call | solution.py:377
  47.1 0.0 copy-done
  47.1 0.6 %copy.5 = f32[4,128]{1,0:T(4,128)} copy(f32[4,128]{1,0:T(4,128)S(1)} %copy-done) | data formatting | bytes 4096
Async XLA Ops:
  38.6 8.5 %copy-start = (f32[4,128]{1,0:T(4,128)S(1)}, f32[4,128]{1,0:T(4,128)}, u32[]{:S(2)}) copy-start(f32[4,128]{1,0:T(4,128)} %get-tuple-element.9) | copy-start | bytes 6148
where the time goes:
time: 47.9 us; the launch traced here: 47.7 us
  Pallas kernels  46.5 us (97%)
  between operations  0.67 us (1%)
  local copies, waits for them, and re-layouts  0.58 us (1%)
    pallas_call x1, Pallas kernels, on_device(): pl.pallas_call(functools.partial(solve_kernel, axes, n), out_shape=[jax.S...  33.3 us
    pallas_call x1, Pallas kernels, on_device(): pl.pallas_call(residual_kernel, out_shape=jax.ShapeDtypeStruct((rows_dev,...  8.52 us
    pallas_call x1, Pallas kernels, on_device(): pl.pallas_call(functools.partial(pick_kernel, axes, n), out_shape=jax.Sha...  4.64 us

commit v1 on v0

v1 whole, which is shorter than its diff:
```python
import functools

import jax
import jax.numpy as jnp
from jax import lax
from jax.experimental import pallas as pl
from jax.experimental.pallas import tpu as pltpu
from jax.sharding import PartitionSpec as P

PRIOR = 192
BLOCK = 8
HIGH = lax.Precision.HIGHEST
MESH = pl.DeviceIdType.MESH
F32 = jnp.float32
BF16 = jnp.bfloat16


def dot(a, b, dims=((1,), (0,))):
    return lax.dot_general(a, b, (dims, ((), ())), precision=HIGH, preferred_element_type=F32)


def halves(value):
    hi = value.astype(BF16)
    return hi, (value - hi.astype(F32)).astype(BF16)


def flat_index(axes):
    (first, _), (second, width) = axes
    return lax.axis_index(first) * width + lax.axis_index(second)


def coords(axes, flat):
    width = axes[1][1]
    return (flat // width, lax.rem(flat, width))


def small_inverse(e):
    size = len(e)
    e = [list(line) for line in e]
    for p in range(size):
        inv = 1.0 / e[p][p]
        line = [e[p][j] * inv for j in range(size)]
        line[p] = -inv
        for i in range(size):
            for j in range(i, size):
                if i == p or j == p:
                    continue
                e[i][j] = e[i][j] - e[p][i] * line[j]
                e[j][i] = e[i][j]
        for j in range(size):
            e[p][j] = line[j]
            e[j][p] = line[j]
    return [[-value for value in line] for line in e]


def sweep_inverse(gram, width=BLOCK):
    size = gram.shape[0]
    shape = (8, size)
    tiles = [gram[8 * t : 8 * t + 8, :] for t in range(size // 8)]
    lane = lax.broadcasted_iota(jnp.int32, shape, 1)
    sub = lax.broadcasted_iota(jnp.int32, shape, 0)
    for k in range(0, size, width):
        t, s = k // 8, k % 8
        inside = (lane >= k) & (lane < k + width)
        own = [jnp.broadcast_to(tiles[t][:, k + q : k + q + 1], shape) for q in range(width)]
        entry = [[None] * width for _ in range(width)]
        for p in range(width):
            for q in range(p, width):
                entry[p][q] = jnp.broadcast_to(own[q][s + p : s + p + 1, :], shape)
                entry[q][p] = entry[p][q]
        small = small_inverse(entry)
        rows = []
        for q in range(width):
            row = jnp.broadcast_to(tiles[t][s + q : s + q + 1, :], shape)
            rows.append(jnp.where(inside, jnp.where(lane == k + q, -1.0, 0.0), row))
        scaled = []
        for p in range(width):
            line = small[p][0] * rows[0]
            for q in range(1, width):
                line = line + small[p][q] * rows[q]
            scaled.append(line)
        fresh = []
        for r in range(size // 8):
            value = jnp.where(inside, 0.0, tiles[r])
            for p in range(width):
                col = own[p] if r == t else jnp.broadcast_to(tiles[r][:, k + p : k + p + 1], shape)
                value = value - col * scaled[p]
            fresh.append(value)
        for p in range(width):
            fresh[t] = jnp.where(sub == s + p, scaled[p], fresh[t])
        tiles = fresh
    return -jnp.concatenate(tiles, axis=0)


def reducers_of(n, tiles):
    count = min(tiles, n // 2)
    return count, n // 4, (n // 2) // count


def solve_kernel(
    axes, n, points_hbm, modes_ref, held, pair, wide_ref, kept_ref, stat_ref,
    points_ref, listed, picked, acc, squares, part1, landed1, own1, full1, part2, landed2, own2, full2,
    local, send1, recv1, share1, gather1, send2, recv2, share2, gather2,
):
    me = flat_index(axes)
    rows_dev, cols = held.shape
    split = cols // 2
    npts = points_ref.shape[0]
    chunks = local.shape[0]
    rows = rows_dev // chunks
    count, first, stride = reducers_of(n, split // 8)
    deep = split // count
    mine = (me - first) // stride
    reduces = (me >= first) & (me < first + count * stride) & (lax.rem(me - first + n, stride) == 0)

    def fetch(c):
        return pltpu.make_async_copy(
            modes_ref.at[pl.ds(c * rows, rows), :], held.at[pl.ds(c * rows, rows), :], local.at[c]
        )

    def loop(body, start, stop):
        def step(i, carry):
            body(i)
            return carry

        lax.fori_loop(start, stop, step, 0)

    points_copy = pltpu.make_async_copy(points_hbm, points_ref, listed)
    points_copy.start()
    loop(lambda c: fetch(c).start(), 0, chunks)
    barrier = pltpu.get_barrier_semaphore()

    def greet(off):
        peer = lax.rem(me + off, n)
        pl.semaphore_signal(barrier, inc=1, device_id=coords(axes, peer), device_id_type=MESH)

    loop(greet, 1, n)
    acc[...] = jnp.zeros_like(acc)
    squares[...] = jnp.zeros_like(squares)

    def grams(c):
        fetch(c).wait()
        at = pl.ds(c * rows, rows)
        fit = held[at, :split]
        rest = held[at, split:]
        f_hi, f_lo = halves(fit)
        r_hi, r_lo = halves(rest)
        pair[at, :split] = f_hi
        pair[at, split:] = f_lo
        left = jnp.concatenate([f_hi, f_lo, r_lo], axis=1)
        right = jnp.concatenate([f_hi, r_hi], axis=1)
        acc[...] += lax.dot_general(left, right, (((0,), (0,)), ((), ())), preferred_element_type=F32)
        squares[...] += jnp.sum((rest * rest).reshape(-1, 8, split), axis=0)

    loop(grams, 0, chunks)

    points_copy.wait()
    base = me * rows_dev

    def take(i):
        at = points_ref[i] - base
        owned = (at >= 0) & (at < rows_dev)
        row = held[pl.ds(jnp.clip(at, 0, rows_dev - 1), 1), :]
        return jnp.where(owned, row, 0.0)

    def pick(t):
        for s in range(8):
            picked[pl.ds(t * 8 + s, 1), :] = take(t * 8 + s)

    picked[...] = jnp.zeros_like(picked)
    loop(pick, 0, npts // 8)
    for i in range(npts // 8 * 8, npts):
        picked[i : i + 1, :] = take(i)
    block = picked[...]
    index = lax.broadcasted_iota(jnp.int32, block.shape, 0)
    chosen = jnp.where(index <= PRIOR, block, 0.0)
    both = dot(chosen[:, :split], chosen, ((0,), (0,)))
    part1[...] = both[:, :split].reshape(part1.shape)

    def peer_copy(src, dst, sent, got, peer):
        return pltpu.make_async_remote_copy(
            src_ref=src, dst_ref=dst, send_sem=sent, recv_sem=got,
            device_id=coords(axes, peer), device_id_type=MESH,
        )

    def scatter(part, landed, sent, got):
        def body(off):
            i = lax.rem(me + off, count)
            peer = first + i * stride

            @pl.when(peer != me)
            def _():
                peer_copy(part.at[i], landed.at[me], sent, got, peer).start()

        loop(body, 0, count)

    def reduce(part, landed, own, full, got, shared, gathered):
        @pl.when(reduces)
        def _():
            seen = landed.at[pl.ds(0, n - 1)]
            peer_copy(seen, seen, shared, got, me).wait_recv()
            landed[me] = part[mine]
            total = landed[0]
            for j in range(1, n):
                total = total + landed[j]
            own[...] = total
            full[mine] = total

            def body(off):
                peer = lax.rem(me + off, n)
                peer_copy(own, full.at[mine], shared, gathered, peer).start()

            loop(body, 1, n)

    def collect(full, shared, gathered):
        for held_here, size in ((reduces, count - 1), (jnp.logical_not(reduces), count)):

            @pl.when(held_here)
            def _():
                seen = full.at[pl.ds(0, size)]
                peer_copy(seen, seen, shared, gathered, me).wait_recv()

    def drain(part, landed, sent, shared):
        for held_here, size in ((reduces, count - 1), (jnp.logical_not(reduces), count)):

            @pl.when(held_here)
            def _():
                seen = part.at[pl.ds(0, size)]
                peer_copy(seen, seen, sent, shared, me).wait_send()

        @pl.when(reduces)
        def _():
            seen = landed.at[pl.ds(0, n - 1)]
            peer_copy(seen, seen, shared, sent, me).wait_send()

    pl.semaphore_wait(barrier, n - 1)
    scatter(part1, landed1, send1, recv1)

    fold = acc[split : 2 * split, :split]
    ftf = acc[:split, :split] + (fold + fold.T)
    ftr = acc[:split, split:] + (acc[split : 2 * split, split:] + acc[2 * split :, :split].T)
    part2[...] = jnp.zeros_like(part2)
    part2[:, 0:deep, :] = both[:, split:].reshape(count, deep, split)
    part2[:, deep : 2 * deep, :] = ftf.reshape(count, deep, split)
    part2[:, 2 * deep : 3 * deep, :] = ftr.reshape(count, deep, split)
    fresh = npts - PRIOR - 1
    tail = slice(3 * deep, 3 * deep + 1)
    for i in range(fresh):
        for half in range(2):
            at = PRIOR + 1 + i
            part2[2 * i + half, tail, :] = picked[at : at + 1, half * split : (half + 1) * split]
    part2[2 * fresh, tail, :] = jnp.sum(squares[...], axis=0, keepdims=True)
    scatter(part2, landed2, send2, recv2)

    reduce(part1, landed1, own1, full1, recv1, share1, gather1)
    reduce(part2, landed2, own2, full2, recv2, share2, gather2)
    collect(full1, share1, gather1)
    gram = full1[...].reshape(split, split)
    inverse = sweep_inverse(gram)
    collect(full2, share2, gather2)
    cross = full2[:, 0:deep, :].reshape(split, split)
    coef = dot(inverse, cross)
    coef = coef + dot(inverse, cross - dot(gram, coef))
    left = [full2[2 * i, tail, :] for i in range(fresh)]
    right = [full2[2 * i + 1, tail, :] for i in range(fresh)]
    lefts = jnp.concatenate(left + [jnp.zeros((8 - fresh, split), F32)], axis=0)
    gains = dot(lefts, inverse)
    errors = dot(lefts, coef)
    ks, ss, ds = [], [], []
    kept = [coef]
    pad7 = jnp.zeros((7, split), F32)
    for j in range(fresh):
        k = gains[j : j + 1, :]
        d = right[j] - errors[j : j + 1, :]
        for k0, s0, d0 in zip(ks, ss, ds):
            along = jnp.sum(k0 * left[j], axis=1, keepdims=True)
            k = k - k0 * (along / s0)
            d = d - along * d0
        s = 1.0 + jnp.sum(k * left[j], axis=1, keepdims=True)
        d = d / s
        ks.append(k)
        ss.append(s)
        ds.append(d)
        turn = dot(jnp.concatenate([k, pad7], axis=0), jnp.concatenate([d, pad7], axis=0), ((0,), (0,)))
        kept.append(kept[-1] + turn)
    c_hi, c_lo = halves(kept[-1])
    wide_ref[0:split, 0:split] = c_hi
    wide_ref[split:, 0:split] = c_hi
    wide_ref[0:split, split:] = c_lo
    wide_ref[split:, split:] = jnp.zeros((split, split), BF16)
    kept_ref[...] = jnp.concatenate(kept, axis=1)
    stat_ref[0:split, 0:split] = full2[:, deep : 2 * deep, :].reshape(split, split)
    stat_ref[0:split, split:] = full2[:, 2 * deep : 3 * deep, :].reshape(split, split)
    stat_ref[split:, 0:split] = jnp.broadcast_to(full2[2 * fresh, tail, :], (8, split))
    stat_ref[split:, split:] = jnp.zeros((8, split), F32)
    drain(part1, landed1, send1, share1)
    drain(part2, landed2, send2, share2)


def residual_kernel(total_rows, held, pair, wide_ref, kept_ref, stat_ref, res_ref, norm_ref, made_buf, wrote):
    chunks, rows, split = made_buf.shape
    steps = norm_ref.shape[0]
    piece = 256 if rows % 256 == 0 else rows

    def flush(c):
        return pltpu.make_async_copy(made_buf.at[c], res_ref.at[pl.ds(c * rows, rows), :], wrote.at[c])

    wide = wide_ref[...]
    for c in range(chunks):
        for at in range(0, rows, piece):
            here = slice(c * rows + at, c * rows + at + piece)
            made = jnp.dot(pair[here, :], wide, preferred_element_type=F32)
            made_buf[c, at : at + piece, :] = held[here, split:] - (made[:, :split] + made[:, split:])
        flush(c).start()
    ftf, ftr = stat_ref[0:split, 0:split], stat_ref[0:split, split:]
    sq = stat_ref[split : split + 1, 0:split]
    curved = dot(ftf, kept_ref[...])
    for j in range(steps):
        cut = slice(j * split, (j + 1) * split)
        bent = kept_ref[:, cut] * (curved[:, cut] - 2.0 * ftr)
        norm_ref[j : j + 1, :] = (sq + jnp.sum(bent, axis=0, keepdims=True)) / total_rows
    for c in range(chunks):
        flush(c).wait()


def on_device(axes, modes, points):
    n = axes[0][1] * axes[1][1]
    rows_dev, cols = modes.shape
    split = cols // 2
    npts = points.shape[0]
    steps = npts - PRIOR
    padded = -(-npts // 8) * 8
    count, _, _ = reducers_of(n, split // 8)
    deep = split // count
    vmem = pl.BlockSpec(memory_space=pltpu.VMEM)
    any_space = pl.BlockSpec(memory_space=pl.ANY)
    chunks = 12 if rows_dev % 96 == 0 else 1

    def buffers(depth):
        return [
            pltpu.VMEM((count, depth, split), F32),
            pltpu.VMEM((n, depth, split), F32),
            pltpu.VMEM((depth, split), F32),
            pltpu.VMEM((count, depth, split), F32),
        ]

    held, pair, wide, kept, stat = pl.pallas_call(
        functools.partial(solve_kernel, axes, n),
        out_shape=[
            pltpu.VMEM((rows_dev, cols), F32),
            pltpu.VMEM((rows_dev, cols), BF16),
            pltpu.VMEM((cols, cols), BF16),
            pltpu.VMEM((split, steps * split), F32),
            pltpu.VMEM((split + 8, cols), F32),
        ],
        in_specs=[pl.BlockSpec(memory_space=pltpu.HBM)] * 2,
        out_specs=[vmem] * 5,
        scratch_shapes=[
            pltpu.SMEM((npts,), jnp.int32),
            pltpu.SemaphoreType.DMA,
            pltpu.VMEM((padded, cols), F32),
            pltpu.VMEM((3 * split, cols), F32),
            pltpu.VMEM((8, split), F32),
        ]
        + buffers(deep)
        + buffers(3 * deep + 1)
        + [pltpu.SemaphoreType.DMA((chunks,))]
        + [pltpu.SemaphoreType.DMA] * 8,
        compiler_params=pltpu.CompilerParams(
            collective_id=0, has_side_effects=True, vmem_limit_bytes=16 * 1024 * 1024
        ),
        name="solve",
    )(pltpu.with_memory_space_constraint(points, pltpu.HBM), pltpu.with_memory_space_constraint(modes, pltpu.HBM))
    residual, norms = pl.pallas_call(
        functools.partial(residual_kernel, rows_dev * n),
        out_shape=[
            jax.ShapeDtypeStruct((rows_dev, split), F32),
            jax.ShapeDtypeStruct((steps, split), F32),
        ],
        in_specs=[vmem] * 5,
        out_specs=[any_space, vmem],
        scratch_shapes=[
            pltpu.VMEM((chunks, rows_dev // chunks, split), F32),
            pltpu.SemaphoreType.DMA((chunks,)),
        ],
        compiler_params=pltpu.CompilerParams(vmem_limit_bytes=16 * 1024 * 1024),
        name="residual",
    )(held, pair, wide, kept, stat)
    return residual, norms


def solution(mesh):
    axes = tuple((name, mesh.shape[name]) for name in ("rows", "grp"))
    return jax.shard_map(
        functools.partial(on_device, axes),
        mesh=mesh,
        in_specs=(P(("rows", "grp"), None), P()),
        out_specs=(P(("rows", "grp"), None), P()),
        check_vma=False,
    )
```

time: 47.9 us -> 32.1 us (0.67)
  Pallas kernels: 46.5 us -> 31.4 us
  local copies, waits for them, and re-layouts: 0.58 us -> 0 us
    pallas_call x3 -> x2, Pallas kernels: 46.5 us -> 31.4 us  [the longest x1 27.7 us: on_device(): pl.pallas_call(functools.partial(solve_kernel, axes, n), out_shape=[pltpu...]
    unnamed x3 -> x0, local copies, waits for them, and re-layouts: 0.58 us -> none
where the time goes in v1:
time: 32.1 us; the launch traced here: 32 us
  Pallas kernels  31.4 us (98%)
  between operations  0.64 us (2%)
    pallas_call x1, Pallas kernels, on_device(): pl.pallas_call(functools.partial(solve_kernel, axes, n), out_shape=[pltpu...  27.7 us
    pallas_call x1, Pallas kernels, on_device(): pl.pallas_call(functools.partial(residual_kernel, rows_dev * n), out_shap...  3.63 us

profile of v1, /device:TPU:0, one launch (start us, length us, event | category | flops | bytes accessed | tf_op | source)
XLA Modules:
  0.0 32.0 jit_solution(17561192775937439580)
XLA Ops:
  0.6 27.7 %solve.1 = (f32[12288,256]{1,0:T(8,128)S(1)}, bf16[12288,256]{1,0:T(8,128)(2,1)S(1)}, bf16[256,256]{1,0:T(8,128)(2,1)S(1)}, f32[128,512]{1,0:T(8,128)S(1)}, f32[136,256]{1,0:T(8,128)S(1)}) custom-call(s32[196]{0:T(256)} %points_hbm.1, f32[12288,256]{1,0:T(8,128)} %modes_ref.1), custom_call_target="tpu_custom_call" | custom-call | tf_op jit(solution)/shard_map/solve/pallas_call | solution.py:347
  28.4 3.6 %residual.1 = (f32[12288,128]{1,0:T(8,128)}, f32[4,128]{1,0:T(4,128)}) custom-call(f32[12288,256]{1,0:T(8,128)S(1)} %get-tuple-element.7.held, bf16[12288,256]{1,0:T(8,128)(2,1)S(1)} %get-tuple-element.8.pair, bf16[256,256]{1,0:T(8,128)(2,1)S(1)} %get-tuple-element.9.wide_ref, f32[128,512]{1,0:T(8,128)S(1)} %get-tuple-element.10.kept_ref, ...), custom_call_target="tpu_custom_call" | custom-call | tf_op jit(solution)/shard_map/residual/pallas_call | solution.py:374

commit v2 on v1

v2 whole, which is shorter than its diff:
```python
import functools

import jax
import jax.numpy as jnp
from jax import lax
from jax.experimental import pallas as pl
from jax.experimental.pallas import tpu as pltpu
from jax.sharding import PartitionSpec as P

PRIOR = 192
BLOCK = 8
HOOK_AT = 32
HIGH = lax.Precision.HIGHEST
LOGICAL = pl.DeviceIdType.LOGICAL
F32 = jnp.float32
BF16 = jnp.bfloat16


def dot(a, b, dims=((1,), (0,))):
    return lax.dot_general(a, b, (dims, ((), ())), precision=HIGH, preferred_element_type=F32)


def halves(value):
    hi = value.astype(BF16)
    return hi, (value - hi.astype(F32)).astype(BF16)


def flat_index(axes):
    (first, _), (second, width) = axes
    return lax.axis_index(first) * width + lax.axis_index(second)


def small_inverse(e):
    size = len(e)
    e = [list(line) for line in e]
    for p in range(size):
        inv = 1.0 / e[p][p]
        line = [e[p][j] * inv for j in range(size)]
        line[p] = -inv
        for i in range(size):
            for j in range(i, size):
                if i == p or j == p:
                    continue
                e[i][j] = e[i][j] - e[p][i] * line[j]
                e[j][i] = e[i][j]
        for j in range(size):
            e[p][j] = line[j]
            e[j][p] = line[j]
    return [[-value for value in line] for line in e]


def sweep_inverse(gram, hook, width=BLOCK):
    size = gram.shape[0]
    shape = (8, size)
    tiles = [gram[8 * t : 8 * t + 8, :] for t in range(size // 8)]
    lane = lax.broadcasted_iota(jnp.int32, shape, 1)
    sub = lax.broadcasted_iota(jnp.int32, shape, 0)
    for k in range(0, size, width):
        if k == HOOK_AT:
            hook()
        t, s = k // 8, k % 8
        inside = (lane >= k) & (lane < k + width)
        own = [jnp.broadcast_to(tiles[t][:, k + q : k + q + 1], shape) for q in range(width)]
        entry = [[None] * width for _ in range(width)]
        for p in range(width):
            for q in range(p, width):
                entry[p][q] = jnp.broadcast_to(own[q][s + p : s + p + 1, :], shape)
                entry[q][p] = entry[p][q]
        small = small_inverse(entry)
        rows = []
        for q in range(width):
            row = jnp.broadcast_to(tiles[t][s + q : s + q + 1, :], shape)
            rows.append(jnp.where(inside, jnp.where(lane == k + q, -1.0, 0.0), row))
        scaled = []
        for p in range(width):
            line = small[p][0] * rows[0]
            for q in range(1, width):
                line = line + small[p][q] * rows[q]
            scaled.append(line)
        fresh = []
        for r in range(size // 8):
            value = jnp.where(inside, 0.0, tiles[r])
            for p in range(width):
                col = own[p] if r == t else jnp.broadcast_to(tiles[r][:, k + p : k + p + 1], shape)
                value = value - col * scaled[p]
            fresh.append(value)
        for p in range(width):
            fresh[t] = jnp.where(sub == s + p, scaled[p], fresh[t])
        tiles = fresh
    return -jnp.concatenate(tiles, axis=0)


def reducers_of(n, tiles):
    count = min(tiles, n // 2)
    return count, n // 4, (n // 2) // count


def solve_kernel(
    axes, n, points_hbm, modes_ref, rest, pair, wide_ref, coef_ref, inverse_ref, stat_ref,
    points_ref, index_ref, fit, picked, acc, squares, part1, landed1, own1, full1, part2, landed2, own2, full2,
    listed, fit_in, rest_in, send1, recv1, share1, gather1, send2, recv2, share2, gather2,
):
    me = flat_index(axes)
    rows_dev, cols = modes_ref.shape
    split = cols // 2
    npts = points_ref.shape[0]
    padded = index_ref.shape[0]
    chunks = fit_in.shape[0]
    rows = rows_dev // chunks
    count, first, stride = reducers_of(n, split // 8)
    deep = split // count
    mine = (me - first) // stride
    reduces = (me >= first) & (me < first + count * stride) & (lax.rem(me - first + n, stride) == 0)

    def fetch_fit(c):
        at = pl.ds(c * rows, rows)
        return pltpu.make_async_copy(modes_ref.at[at, pl.ds(0, split)], fit.at[at, :], fit_in.at[c])

    def fetch_rest(c):
        at = pl.ds(c * rows, rows)
        return pltpu.make_async_copy(modes_ref.at[at, pl.ds(split, split)], rest.at[at, :], rest_in.at[c])

    def loop(body, start, stop, unroll=1):
        def step(i, carry):
            body(i)
            return carry

        lax.fori_loop(start, stop, step, 0, unroll=unroll)

    points_copy = pltpu.make_async_copy(points_hbm, points_ref, listed)
    points_copy.start()
    for c in range(chunks):
        fetch_fit(c).start()
    barrier = pltpu.get_barrier_semaphore()

    def greet(off):
        peer = lax.rem(me + off, n)
        pl.semaphore_signal(barrier, inc=1, device_id=peer, device_id_type=LOGICAL)

    loop(greet, 1, n)
    for c in range(chunks):
        fetch_rest(c).start()
    fit[rows_dev:, :] = jnp.zeros((8, split), F32)
    rest[rows_dev:, :] = jnp.zeros((8, split), F32)
    acc[...] = jnp.zeros_like(acc)
    squares[...] = jnp.zeros_like(squares)
    points_copy.wait()
    base = me * rows_dev

    def locate(i):
        at = points_ref[i] - base
        index_ref[i] = jnp.where((at >= 0) & (at < rows_dev), at, rows_dev)

    loop(locate, 0, npts, 4)
    for i in range(npts, padded):
        index_ref[i] = rows_dev

    def fit_gram(c):
        fetch_fit(c).wait()
        at = pl.ds(c * rows, rows)
        hi, lo = halves(fit[at, :])
        pair[at, :split] = hi
        pair[at, split:] = lo
        both = jnp.concatenate([hi, lo], axis=1)
        acc[:, :split] += lax.dot_general(both, hi, (((0,), (0,)), ((), ())), preferred_element_type=F32)

    def rest_gram(c):
        fetch_rest(c).wait()
        at = pl.ds(c * rows, rows)
        value = rest[at, :]
        hi, lo = halves(value)
        both = jnp.concatenate([hi, lo], axis=1)
        acc[:, split:] += lax.dot_general(pair[at, :], both, (((0,), (0,)), ((), ())), preferred_element_type=F32)
        squares[...] += jnp.sum((value * value).reshape(-1, 8, split), axis=0)

    def take(source, half):
        def pick(t):
            for s in range(8):
                picked[half, t, s : s + 1, :] = source[pl.ds(index_ref[t * 8 + s], 1), :]

        loop(pick, 0, padded // 8)

    def peer_copy(src, dst, sent, got, peer):
        return pltpu.make_async_remote_copy(
            src_ref=src, dst_ref=dst, send_sem=sent, recv_sem=got,
            device_id=peer, device_id_type=LOGICAL,
        )

    def scatter(part, landed, sent, got):
        def body(off):
            i = lax.rem(me + off, count)
            peer = first + i * stride

            @pl.when(peer != me)
            def _():
                peer_copy(part.at[i], landed.at[me], sent, got, peer).start()

        loop(body, 0, count)

    def reduce(part, landed, own, full, got, shared, gathered):
        @pl.when(reduces)
        def _():
            seen = landed.at[pl.ds(0, n - 1)]
            peer_copy(seen, seen, shared, got, me).wait_recv()
            landed[me] = part[mine]
            total = landed[0]
            for j in range(1, n):
                total = total + landed[j]
            own[...] = total
            full[mine] = total

            def body(off):
                peer = lax.rem(me + off, n)
                peer_copy(own, full.at[mine], shared, gathered, peer).start()

            loop(body, 1, n)

    def collect(full, shared, gathered):
        for held_here, size in ((reduces, count - 1), (jnp.logical_not(reduces), count)):

            @pl.when(held_here)
            def _():
                seen = full.at[pl.ds(0, size)]
                peer_copy(seen, seen, shared, gathered, me).wait_recv()

    def drain(part, landed, sent, shared):
        for held_here, size in ((reduces, count - 1), (jnp.logical_not(reduces), count)):

            @pl.when(held_here)
            def _():
                seen = part.at[pl.ds(0, size)]
                peer_copy(seen, seen, sent, shared, me).wait_send()

        @pl.when(reduces)
        def _():
            seen = landed.at[pl.ds(0, n - 1)]
            peer_copy(seen, seen, shared, sent, me).wait_send()

    with jax.named_scope("fgram"):
        loop(fit_gram, 0, chunks)
    with jax.named_scope("fpick"):
        take(fit, 0)
    with jax.named_scope("fdot"):
        left = picked[0].reshape(padded, split)
        part1[...] = dot(left, left, ((0,), (0,))).reshape(part1.shape)
    with jax.named_scope("barrier"):
        pl.semaphore_wait(barrier, n - 1)
    with jax.named_scope("scat1"):
        scatter(part1, landed1, send1, recv1)

    with jax.named_scope("rgram"):
        loop(rest_gram, 0, chunks)
    with jax.named_scope("rpick"):
        take(rest, 1)
    with jax.named_scope("rdot"):
        cross = dot(picked[0].reshape(padded, split), picked[1].reshape(padded, split), ((0,), (0,)))
        fold = acc[split:, :split]
        ftf = acc[:split, :split] + (fold + fold.T)
        ftr = acc[:split, split:cols] + (acc[:split, cols:] + acc[split:, split:cols])
        part2[...] = jnp.zeros_like(part2)
        part2[:, 0:deep, :] = cross.reshape(count, deep, split)
        part2[:, deep : 2 * deep, :] = ftf.reshape(count, deep, split)
        part2[:, 2 * deep : 3 * deep, :] = ftr.reshape(count, deep, split)
        fresh = npts - PRIOR - 1
        tail = slice(3 * deep, 3 * deep + 1)
        for i in range(fresh):
            for half in range(2):
                at = PRIOR + 1 + i
                part2[2 * i + half, tail, :] = picked[half, at // 8, at % 8 : at % 8 + 1, :]
        part2[2 * fresh, tail, :] = jnp.sum(squares[...], axis=0, keepdims=True)
    with jax.named_scope("scat2"):
        scatter(part2, landed2, send2, recv2)

    with jax.named_scope("red1"):
        reduce(part1, landed1, own1, full1, recv1, share1, gather1)
    with jax.named_scope("col1"):
        collect(full1, share1, gather1)

    def hook():
        with jax.named_scope("red2"):
            reduce(part2, landed2, own2, full2, recv2, share2, gather2)

    with jax.named_scope("sweep"):
        inverse = sweep_inverse(full1[...].reshape(split, split), hook)
    with jax.named_scope("col2"):
        collect(full2, share2, gather2)
    with jax.named_scope("coef"):
        coef = dot(inverse, full2[:, 0:deep, :].reshape(split, split))
        c_hi, c_lo = halves(coef)
        wide_ref[0:split, 0:split] = c_hi
        wide_ref[split:, 0:split] = c_hi
        wide_ref[0:split, split:] = c_lo
        wide_ref[split:, split:] = jnp.zeros((split, split), BF16)
        coef_ref[...] = coef
        inverse_ref[...] = inverse
        stat_ref[0:split, 0:split] = full2[:, deep : 2 * deep, :].reshape(split, split)
        stat_ref[0:split, split:] = full2[:, 2 * deep : 3 * deep, :].reshape(split, split)
        zero = jnp.zeros((8 - fresh, split), F32)
        for half in range(2):
            lines = [full2[2 * i + half, tail, :] for i in range(fresh)]
            stat_ref[split : split + 8, half * split : (half + 1) * split] = jnp.concatenate(lines + [zero], axis=0)
        stat_ref[split + 8 :, 0:split] = jnp.broadcast_to(full2[2 * fresh, tail, :], (8, split))
        stat_ref[split + 8 :, split:] = jnp.zeros((8, split), F32)
    with jax.named_scope("drain"):
        drain(part1, landed1, send1, share1)
        drain(part2, landed2, send2, share2)


def residual_kernel(
    total_rows, rest, pair, wide_ref, coef_ref, inverse_ref, stat_ref, res_ref, norm_ref, made_buf, norm_buf, wrote, normed
):
    chunks, rows, split = made_buf.shape
    steps = norm_buf.shape[0]
    fresh = steps - 1
    piece = 256 if rows % 256 == 0 else rows

    def flush(c):
        return pltpu.make_async_copy(made_buf.at[c], res_ref.at[pl.ds(c * rows, rows), :], wrote.at[c])

    wide = wide_ref[...]
    for c in range(chunks):
        for at in range(0, rows, piece):
            here = slice(c * rows + at, c * rows + at + piece)
            made = jnp.dot(pair[here, :], wide, preferred_element_type=F32)
            made_buf[c, at : at + piece, :] = rest[here, :] - (made[:, :split] + made[:, split:])
        flush(c).start()
    with jax.named_scope("chain"):
        coef = coef_ref[...]
        lefts = stat_ref[split : split + 8, 0:split]
        gains = dot(lefts, inverse_ref[...])
        errors = stat_ref[split : split + 8, split:] - dot(lefts, coef)
        kept = [coef]
        done = []
        pad7 = jnp.zeros((7, split), F32)
        for j in reversed(range(fresh)):
            left = lefts[j : j + 1, :]
            k = gains[j : j + 1, :]
            d = errors[j : j + 1, :]
            for k0, s0, d0 in done:
                along = jnp.sum(k0 * left, axis=1, keepdims=True)
                k = k + k0 * (along / s0)
                d = d + along * d0
            s = 1.0 - jnp.sum(k * left, axis=1, keepdims=True)
            d = d / s
            done.append((k, s, d))
            turn = dot(jnp.concatenate([k, pad7], axis=0), jnp.concatenate([d, pad7], axis=0), ((0,), (0,)))
            kept.append(kept[-1] - turn)
        kept = kept[::-1]
    with jax.named_scope("curved"):
        ftf, ftr = stat_ref[0:split, 0:split], stat_ref[0:split, split:]
        sq = stat_ref[split + 8 : split + 9, 0:split]
        curved = dot(ftf, jnp.concatenate(kept, axis=1))
        for j in range(steps):
            bent = kept[j] * (curved[:, j * split : (j + 1) * split] - 2.0 * ftr)
            norm_buf[j : j + 1, :] = (sq + jnp.sum(bent, axis=0, keepdims=True)) / total_rows
    norm_copy = pltpu.make_async_copy(norm_buf, norm_ref, normed)
    norm_copy.start()
    with jax.named_scope("flushwait"):
        for c in range(chunks):
            flush(c).wait()
        norm_copy.wait()


def on_device(axes, modes, points):
    n = axes[0][1] * axes[1][1]
    rows_dev, cols = modes.shape
    split = cols // 2
    npts = points.shape[0]
    steps = npts - PRIOR
    padded = -(-npts // 8) * 8
    count, _, _ = reducers_of(n, split // 8)
    deep = split // count
    vmem = pl.BlockSpec(memory_space=pltpu.VMEM)
    in_chunks = 6 if rows_dev % 96 == 0 else 1
    out_chunks = 12 if rows_dev % 96 == 0 else 1

    def buffers(depth):
        return [
            pltpu.VMEM((count, depth, split), F32),
            pltpu.VMEM((n, depth, split), F32),
            pltpu.VMEM((depth, split), F32),
            pltpu.VMEM((count, depth, split), F32),
        ]

    hbm = pl.BlockSpec(memory_space=pltpu.HBM)
    rest, pair, wide, coef, inverse, stat = pl.pallas_call(
        functools.partial(solve_kernel, axes, n),
        out_shape=[
            pltpu.VMEM((rows_dev + 8, split), F32),
            pltpu.VMEM((rows_dev, cols), BF16),
            pltpu.VMEM((cols, cols), BF16),
            pltpu.VMEM((split, split), F32),
            pltpu.VMEM((split, split), F32),
            pltpu.VMEM((split + 16, cols), F32),
        ],
        in_specs=[hbm] * 2,
        out_specs=[vmem] * 6,
        scratch_shapes=[
            pltpu.SMEM((npts,), jnp.int32),
            pltpu.SMEM((padded,), jnp.int32),
            pltpu.VMEM((rows_dev + 8, split), F32),
            pltpu.VMEM((2, padded // 8, 8, split), F32),
            pltpu.VMEM((cols, 3 * split), F32),
            pltpu.VMEM((8, split), F32),
        ]
        + buffers(deep)
        + buffers(3 * deep + 1)
        + [pltpu.SemaphoreType.DMA]
        + [pltpu.SemaphoreType.DMA((in_chunks,))] * 2
        + [pltpu.SemaphoreType.DMA] * 8,
        compiler_params=pltpu.CompilerParams(
            collective_id=0, has_side_effects=True, vmem_limit_bytes=24 * 1024 * 1024
        ),
        name="solve",
    )(pltpu.with_memory_space_constraint(points, pltpu.HBM), pltpu.with_memory_space_constraint(modes, pltpu.HBM))
    residual, norms = pl.pallas_call(
        functools.partial(residual_kernel, rows_dev * n),
        out_shape=[
            jax.ShapeDtypeStruct((rows_dev, split), F32),
            jax.ShapeDtypeStruct((steps, split), F32),
        ],
        in_specs=[vmem] * 6,
        out_specs=[hbm, hbm],
        scratch_shapes=[
            pltpu.VMEM((out_chunks, rows_dev // out_chunks, split), F32),
            pltpu.VMEM((steps, split), F32),
            pltpu.SemaphoreType.DMA((out_chunks,)),
            pltpu.SemaphoreType.DMA,
        ],
        compiler_params=pltpu.CompilerParams(vmem_limit_bytes=16 * 1024 * 1024),
        name="residual",
    )(rest, pair, wide, coef, inverse, stat)
    return residual, norms


def solution(mesh):
    axes = tuple((name, mesh.shape[name]) for name in ("rows", "grp"))
    return jax.shard_map(
        functools.partial(on_device, axes),
        mesh=mesh,
        in_specs=(P(("rows", "grp"), None), P()),
        out_specs=(P(("rows", "grp"), None), P()),
        check_vma=False,
    )
```

time: 32.1 us -> 30.4 us (0.947)
  Pallas kernels: 31.4 us -> 29.6 us
    pallas_call x1, Pallas kernels: 27.7 us -> 26.2 us  [on_device(): pl.pallas_call(functools.partial(solve_kernel, axes, n), out_shape=[pltpu...]
where the time goes in v2:
time: 30.4 us; the launch traced here: 30.3 us
  Pallas kernels  29.6 us (97%)
  between operations  0.64 us (2%)
    pallas_call x1, Pallas kernels, on_device(): pl.pallas_call(functools.partial(solve_kernel, axes, n), out_shape=[pltpu...  26.2 us
    pallas_call x1, Pallas kernels, on_device(): pl.pallas_call(functools.partial(residual_kernel, rows_dev * n), out_shap...  3.38 us

profile of v2, /device:TPU:0, one launch (start us, length us, event | category | flops | bytes accessed | tf_op | source)
XLA Modules:
  0.0 30.3 jit_solution(16660896242647089191)
XLA Ops:
  0.6 26.2 %solve.1 = (f32[12296,128]{1,0:T(8,128)S(1)}, bf16[12288,256]{1,0:T(8,128)(2,1)S(1)}, bf16[256,256]{1,0:T(8,128)(2,1)S(1)}, f32[128,128]{1,0:T(8,128)S(1)}, f32[...) custom-call(s32[196]{0:T(256)} %points_hbm.1, f32[12288,256]{1,0:T(8,128)} %modes_ref.1), custom_call_target="tpu_custom_call" | custom-call | tf_op jit(solution)/shard_map/solve/pallas_call | solution.py:386
  26.9 3.4 %residual.1 = (f32[12288,128]{1,0:T(8,128)}, f32[4,128]{1,0:T(4,128)}) custom-call(f32[12296,128]{1,0:T(8,128)S(1)} %get-tuple-element.8.rest, bf16[12288,256]{1,0:T(8,128)(2,1)S(1)} %get-tuple-element.9.pair, bf16[256,256]{1,0:T(8,128)(2,1)S(1)} %get-tuple-element.10.wide_ref, f32[128,128]{1,0:T(8,128)S(1)} %get-tuple-element.11.coef_ref, ...), custom_call_target="tpu_custom_call" | custom-call | tf_op jit(solution)/shard_map/residual/pallas_call | solution.py:416

commit v3 on v2

--- a/solution.py
+++ b/solution.py
@@ -9,7 +9,8 @@
 
 PRIOR = 192
 BLOCK = 8
-HOOK_AT = 32
+HOOK_FIT, HOOK_REST = 8, 24
+WAVE = 1
 HIGH = lax.Precision.HIGHEST
 LOGICAL = pl.DeviceIdType.LOGICAL
 F32 = jnp.float32
@@ -56,8 +57,7 @@
     lane = lax.broadcasted_iota(jnp.int32, shape, 1)
     sub = lax.broadcasted_iota(jnp.int32, shape, 0)
     for k in range(0, size, width):
-        if k == HOOK_AT:
-            hook()
+        hook(k)
         t, s = k // 8, k % 8
         inside = (lane >= k) & (lane < k + width)
         own = [jnp.broadcast_to(tiles[t][:, k + q : k + q + 1], shape) for q in range(width)]
@@ -91,14 +91,15 @@
 
 
 def reducers_of(n, tiles):
-    count = min(tiles, n // 2)
-    return count, n // 4, (n // 2) // count
+    count = min(tiles // 2, n // 4)
+    return count, n // 4 + 1, (n // 2) // count
 
 
 def solve_kernel(
     axes, n, points_hbm, modes_ref, rest, pair, wide_ref, coef_ref, inverse_ref, stat_ref,
-    points_ref, index_ref, fit, picked, acc, squares, part1, landed1, own1, full1, part2, landed2, own2, full2,
-    listed, fit_in, rest_in, send1, recv1, share1, gather1, send2, recv2, share2, gather2,
+    points_ref, index_ref, fit, turned, picked, acc1, acc2, squares,
+    part1, landed1, own1, full1, part2, landed2, own2, full2, part3, landed3, own3, full3,
+    listed, fit_in, rest_in, send1, recv1, share1, gather1, send2, recv2, share2, gather2, send3, recv3, share3, gather3,
 ):
     me = flat_index(axes)
     rows_dev, cols = modes_ref.shape
@@ -142,8 +143,8 @@
         fetch_rest(c).start()
     fit[rows_dev:, :] = jnp.zeros((8, split), F32)
     rest[rows_dev:, :] = jnp.zeros((8, split), F32)
-    acc[...] = jnp.zeros_like(acc)
-    squares[...] = jnp.zeros_like(squares)
+    for total in (acc1, acc2, squares):
+        total[...] = jnp.zeros_like(total)
     points_copy.wait()
     base = me * rows_dev
 
@@ -155,23 +156,31 @@
     for i in range(npts, padded):
         index_ref[i] = rows_dev
 
+    wave = WAVE if chunks % WAVE == 0 else 1
+    plain = (((1,), (0,)), ((), ()))
+
+    def pieces_of(c):
+        size = wave * rows // 2
+        return [(i, slice(c * wave * rows + i * size, c * wave * rows + (i + 1) * size)) for i in range(2)]
+
     def fit_gram(c):
-        fetch_fit(c).wait()
-        at = pl.ds(c * rows, rows)
-        hi, lo = halves(fit[at, :])
-        pair[at, :split] = hi
-        pair[at, split:] = lo
-        both = jnp.concatenate([hi, lo], axis=1)
-        acc[:, :split] += lax.dot_general(both, hi, (((0,), (0,)), ((), ())), preferred_element_type=F32)
+        for i, at in pieces_of(c):
+            hi, lo = halves(fit[at, :])
+            pair[at, :split] = hi
+            pair[at, split:] = lo
+            flip = hi.T
+            turned[:, at] = flip
+            acc1[i] += lax.dot_general(flip, jnp.concatenate([hi, lo], axis=1), plain, preferred_element_type=F32)
 
     def rest_gram(c):
-        fetch_rest(c).wait()
-        at = pl.ds(c * rows, rows)
-        value = rest[at, :]
-        hi, lo = halves(value)
-        both = jnp.concatenate([hi, lo], axis=1)
-        acc[:, split:] += lax.dot_general(pair[at, :], both, (((0,), (0,)), ((), ())), preferred_element_type=F32)
-        squares[...] += jnp.sum((value * value).reshape(-1, 8, split), axis=0)
+        for i in range(wave):
+            fetch_rest(c * wave + i).wait()
+        for i, at in pieces_of(c):
+            value = rest[at, :]
+            hi, lo = halves(value)
+            both = jnp.concatenate([turned[:, at], pair[at, split:].T], axis=0)
+            acc2[i] += lax.dot_general(both, jnp.concatenate([hi, lo], axis=1), plain, preferred_element_type=F32)
+            squares[...] += jnp.sum((value * value).reshape(-1, 8, split), axis=0)
 
     def take(source, half):
         def pick(t):
@@ -197,17 +206,20 @@
 
         loop(body, 0, count)
 
-    def reduce(part, landed, own, full, got, shared, gathered):
+    def reduce(pieces, own, full, shared, gathered):
         @pl.when(reduces)
         def _():
-            seen = landed.at[pl.ds(0, n - 1)]
-            peer_copy(seen, seen, shared, got, me).wait_recv()
-            landed[me] = part[mine]
-            total = landed[0]
-            for j in range(1, n):
-                total = total + landed[j]
-            own[...] = total
-            full[mine] = total
+            at = 0
+            for part, landed, got in pieces:
+                seen = landed.at[pl.ds(0, n - 1)]
+                peer_copy(seen, seen, shared, got, me).wait_recv()
+                landed[me] = part[mine]
+                total = landed[0]
+                for j in range(1, n):
+                    total = total + landed[j]
+                own[at : at + total.shape[0], :] = total
+                at += total.shape[0]
+            full[mine] = own[...]
 
             def body(off):
                 peer = lax.rem(me + off, n)
@@ -223,21 +235,30 @@
                 seen = full.at[pl.ds(0, size)]
                 peer_copy(seen, seen, shared, gathered, me).wait_recv()
 
-    def drain(part, landed, sent, shared):
+    def drain(parts, full, shared):
         for held_here, size in ((reduces, count - 1), (jnp.logical_not(reduces), count)):
 
             @pl.when(held_here)
             def _():
-                seen = part.at[pl.ds(0, size)]
-                peer_copy(seen, seen, sent, shared, me).wait_send()
+                for part, sent in parts:
+                    seen = part.at[pl.ds(0, size)]
+                    peer_copy(seen, seen, sent, shared, me).wait_send()
 
         @pl.when(reduces)
         def _():
-            seen = landed.at[pl.ds(0, n - 1)]
-            peer_copy(seen, seen, shared, sent, me).wait_send()
-
+            seen = full.at[pl.ds(0, count)]
+            for _ in range((n - 1) // count):
+                peer_copy(seen, seen, shared, shared, me).wait_send()
+            rest_of = full.at[pl.ds(0, (n - 1) % count)]
+            peer_copy(rest_of, rest_of, shared, shared, me).wait_send()
+
+    waves = chunks // wave
     with jax.named_scope("fgram"):
-        loop(fit_gram, 0, chunks)
+        for c in range(waves):
+            for i in range(wave):
+                fetch_fit(c * wave + i).wait()
+            if c < waves - 1:
+                fit_gram(c)
     with jax.named_scope("fpick"):
         take(fit, 0)
     with jax.named_scope("fdot"):
@@ -248,44 +269,55 @@
     with jax.named_scope("scat1"):
         scatter(part1, landed1, send1, recv1)
 
-    with jax.named_scope("rgram"):
-        loop(rest_gram, 0, chunks)
+    with jax.named_scope("fgram2"):
+        fit_gram(waves - 1)
+    for c in range(waves):
+        with jax.named_scope("rgram"):
+            rest_gram(c)
+        if c == 0:
+            with jax.named_scope("scat2"):
+                total = acc1[0] + acc1[1]
+                cross = total[:, split:]
+                part2[...] = (total[:, :split] + (cross + cross.T)).reshape(part2.shape)
+                scatter(part2, landed2, send2, recv2)
     with jax.named_scope("rpick"):
         take(rest, 1)
     with jax.named_scope("rdot"):
         cross = dot(picked[0].reshape(padded, split), picked[1].reshape(padded, split), ((0,), (0,)))
-        fold = acc[split:, :split]
-        ftf = acc[:split, :split] + (fold + fold.T)
-        ftr = acc[:split, split:cols] + (acc[:split, cols:] + acc[split:, split:cols])
-        part2[...] = jnp.zeros_like(part2)
-        part2[:, 0:deep, :] = cross.reshape(count, deep, split)
-        part2[:, deep : 2 * deep, :] = ftf.reshape(count, deep, split)
-        part2[:, 2 * deep : 3 * deep, :] = ftr.reshape(count, deep, split)
+        total = acc2[0] + acc2[1]
+        ftr = total[:split, :split] + (total[:split, split:] + total[split:, :split])
         fresh = npts - PRIOR - 1
-        tail = slice(3 * deep, 3 * deep + 1)
+        tail = slice(2 * deep, 2 * deep + 1)
+        part3[:, tail, :] = jnp.zeros((count, 1, split), F32)
+        part3[:, 0:deep, :] = cross.reshape(count, deep, split)
+        part3[:, deep : 2 * deep, :] = ftr.reshape(count, deep, split)
         for i in range(fresh):
             for half in range(2):
                 at = PRIOR + 1 + i
-                part2[2 * i + half, tail, :] = picked[half, at // 8, at % 8 : at % 8 + 1, :]
-        part2[2 * fresh, tail, :] = jnp.sum(squares[...], axis=0, keepdims=True)
-    with jax.named_scope("scat2"):
-        scatter(part2, landed2, send2, recv2)
+                part3[2 * i + half, tail, :] = picked[half, at // 8, at % 8 : at % 8 + 1, :]
+        part3[2 * fresh, tail, :] = jnp.sum(squares[...], axis=0, keepdims=True)
+    with jax.named_scope("scat3"):
+        scatter(part3, landed3, send3, recv3)
 
     with jax.named_scope("red1"):
-        reduce(part1, landed1, own1, full1, recv1, share1, gather1)
+        reduce([(part1, landed1, recv1)], own1, full1, share1, gather1)
     with jax.named_scope("col1"):
         collect(full1, share1, gather1)
 
-    def hook():
-        with jax.named_scope("red2"):
-            reduce(part2, landed2, own2, full2, recv2, share2, gather2)
+    def hook(k):
+        if k == HOOK_FIT:
+            with jax.named_scope("red2"):
+                reduce([(part2, landed2, recv2)], own2, full2, share2, gather2)
+        if k == HOOK_REST:
+            with jax.named_scope("red3"):
+                reduce([(part3, landed3, recv3)], own3, full3, share3, gather3)
 
     with jax.named_scope("sweep"):
         inverse = sweep_inverse(full1[...].reshape(split, split), hook)
-    with jax.named_scope("col2"):
-        collect(full2, share2, gather2)
+    with jax.named_scope("col3"):
+        collect(full3, share3, gather3)
     with jax.named_scope("coef"):
-        coef = dot(inverse, full2[:, 0:deep, :].reshape(split, split))
+        coef = dot(inverse, full3[:, 0:deep, :].reshape(split, split))
         c_hi, c_lo = halves(coef)
         wide_ref[0:split, 0:split] = c_hi
         wide_ref[split:, 0:split] = c_hi
@@ -293,17 +325,20 @@
         wide_ref[split:, split:] = jnp.zeros((split, split), BF16)
         coef_ref[...] = coef
         inverse_ref[...] = inverse
-        stat_ref[0:split, 0:split] = full2[:, deep : 2 * deep, :].reshape(split, split)
-        stat_ref[0:split, split:] = full2[:, 2 * deep : 3 * deep, :].reshape(split, split)
+        stat_ref[0:split, split:] = full3[:, deep : 2 * deep, :].reshape(split, split)
         zero = jnp.zeros((8 - fresh, split), F32)
         for half in range(2):
-            lines = [full2[2 * i + half, tail, :] for i in range(fresh)]
+            lines = [full3[2 * i + half, tail, :] for i in range(fresh)]
             stat_ref[split : split + 8, half * split : (half + 1) * split] = jnp.concatenate(lines + [zero], axis=0)
-        stat_ref[split + 8 :, 0:split] = jnp.broadcast_to(full2[2 * fresh, tail, :], (8, split))
+        stat_ref[split + 8 :, 0:split] = jnp.broadcast_to(full3[2 * fresh, tail, :], (8, split))
         stat_ref[split + 8 :, split:] = jnp.zeros((8, split), F32)
+    with jax.named_scope("col2"):
+        collect(full2, share2, gather2)
+        stat_ref[0:split, 0:split] = full2[...].reshape(split, split)
     with jax.named_scope("drain"):
-        drain(part1, landed1, send1, share1)
-        drain(part2, landed2, send2, share2)
+        drain([(part1, send1)], full1, share1)
+        drain([(part2, send2)], full2, share2)
+        drain([(part3, send3)], full3, share3)
 
 
 def residual_kernel(
@@ -374,13 +409,11 @@
     in_chunks = 6 if rows_dev % 96 == 0 else 1
     out_chunks = 12 if rows_dev % 96 == 0 else 1
 
-    def buffers(depth):
-        return [
-            pltpu.VMEM((count, depth, split), F32),
-            pltpu.VMEM((n, depth, split), F32),
-            pltpu.VMEM((depth, split), F32),
-            pltpu.VMEM((count, depth, split), F32),
-        ]
+    def sources(depth):
+        return [pltpu.VMEM((count, depth, split), F32), pltpu.VMEM((n, depth, split), F32)]
+
+    def sums(depth):
+        return [pltpu.VMEM((depth, split), F32), pltpu.VMEM((count, depth, split), F32)]
 
     hbm = pl.BlockSpec(memory_space=pltpu.HBM)
     rest, pair, wide, coef, inverse, stat = pl.pallas_call(
@@ -399,15 +432,21 @@
             pltpu.SMEM((npts,), jnp.int32),
             pltpu.SMEM((padded,), jnp.int32),
             pltpu.VMEM((rows_dev + 8, split), F32),
+            pltpu.VMEM((split, rows_dev), BF16),
             pltpu.VMEM((2, padded // 8, 8, split), F32),
-            pltpu.VMEM((cols, 3 * split), F32),
+            pltpu.VMEM((2, split, cols), F32),
+            pltpu.VMEM((2, cols, cols), F32),
             pltpu.VMEM((8, split), F32),
         ]
-        + buffers(deep)
-        + buffers(3 * deep + 1)
+        + sources(deep)
+        + sums(deep)
+        + sources(deep)
+        + sums(deep)
+        + sources(2 * deep + 1)
+        + sums(2 * deep + 1)
         + [pltpu.SemaphoreType.DMA]
         + [pltpu.SemaphoreType.DMA((in_chunks,))] * 2
-        + [pltpu.SemaphoreType.DMA] * 8,
+        + [pltpu.SemaphoreType.DMA] * 12,
         compiler_params=pltpu.CompilerParams(
             collective_id=0, has_side_effects=True, vmem_limit_bytes=24 * 1024 * 1024
         ),

time: 30.4 us -> 28 us (0.921)
  Pallas kernels: 29.6 us -> 27.2 us
    pallas_call x1, Pallas kernels: 26.2 us -> 23.8 us  [on_device(): pl.pallas_call(functools.partial(solve_kernel, axes, n), out_shape=[pltpu...]
where the time goes in v3:
time: 28 us; the launch traced here: 27.8 us
  Pallas kernels  27.2 us (97%)
  between operations  0.64 us (2%)
    pallas_call x1, Pallas kernels, on_device(): pl.pallas_call(functools.partial(solve_kernel, axes, n), out_shape=[pltpu...  23.8 us
    pallas_call x1, Pallas kernels, on_device(): pl.pallas_call(functools.partial(residual_kernel, rows_dev * n), out_shap...  3.38 us

profile of v3, /device:TPU:0, one launch (start us, length us, event | category | flops | bytes accessed | tf_op | source)
XLA Modules:
  0.0 27.8 jit_solution(5212149193315820383)
XLA Ops:
  0.6 23.8 %solve.1 = (f32[12296,128]{1,0:T(8,128)S(1)}, bf16[12288,256]{1,0:T(8,128)(2,1)S(1)}, bf16[256,256]{1,0:T(8,128)(2,1)S(1)}, f32[128,128]{1,0:T(8,128)S(1)}, f32[...) custom-call(s32[196]{0:T(256)} %points_hbm.1, f32[12288,256]{1,0:T(8,128)} %modes_ref.1), custom_call_target="tpu_custom_call" | custom-call | tf_op jit(solution)/shard_map/solve/pallas_call | solution.py:419
  24.4 3.4 %residual.1 = (f32[12288,128]{1,0:T(8,128)}, f32[4,128]{1,0:T(4,128)}) custom-call(f32[12296,128]{1,0:T(8,128)S(1)} %get-tuple-element.8.rest, bf16[12288,256]{1,0:T(8,128)(2,1)S(1)} %get-tuple-element.9.pair, bf16[256,256]{1,0:T(8,128)(2,1)S(1)} %get-tuple-element.10.wide_ref, f32[128,128]{1,0:T(8,128)S(1)} %get-tuple-element.11.coef_ref, ...), custom_call_target="tpu_custom_call" | custom-call | tf_op jit(solution)/shard_map/residual/pallas_call | solution.py:455

commit v4 on v3

--- a/solution.py
+++ b/solution.py
@@ -8,9 +8,10 @@
 from jax.sharding import PartitionSpec as P
 
 PRIOR = 192
-BLOCK = 8
-HOOK_FIT, HOOK_REST = 8, 24
+HOOK_REST, HOOK_FIT = 8, 24
 WAVE = 1
+UNROLL = 8
+SEND_FIT = 3
 HIGH = lax.Precision.HIGHEST
 LOGICAL = pl.DeviceIdType.LOGICAL
 F32 = jnp.float32
@@ -50,42 +51,51 @@
     return [[-value for value in line] for line in e]
 
 
-def sweep_inverse(gram, hook, width=BLOCK):
+def added(terms):
+    while len(terms) > 1:
+        pairs = [terms[i] + terms[i + 1] for i in range(0, len(terms) - 1, 2)]
+        terms = pairs + terms[len(pairs) * 2 :]
+    return terms[0]
+
+
+def sweep_inverse(gram, hook, line_ref, column_ref):
     size = gram.shape[0]
+    steps = size // 8
     shape = (8, size)
-    tiles = [gram[8 * t : 8 * t + 8, :] for t in range(size // 8)]
+    wide = (8, line_ref.shape[-1])
+    tiles = [gram[8 * t : 8 * t + 8, :] for t in range(steps)]
     lane = lax.broadcasted_iota(jnp.int32, shape, 1)
     sub = lax.broadcasted_iota(jnp.int32, shape, 0)
-    for k in range(0, size, width):
+
+    def column(tile, at):
+        return jnp.broadcast_to(tile[:, at : at + 1], shape)
+
+    for t in range(steps):
+        k = 8 * t
         hook(k)
-        t, s = k // 8, k % 8
-        inside = (lane >= k) & (lane < k + width)
-        own = [jnp.broadcast_to(tiles[t][:, k + q : k + q + 1], shape) for q in range(width)]
-        entry = [[None] * width for _ in range(width)]
-        for p in range(width):
-            for q in range(p, width):
-                entry[p][q] = jnp.broadcast_to(own[q][s + p : s + p + 1, :], shape)
+        own = [column(tiles[t], k + q) for q in range(8)]
+        line_ref[t, :, 0:size] = tiles[t]
+        for q in range(8):
+            column_ref[t, q, :, 0:size] = own[q]
+        entry = [[None] * 8 for _ in range(8)]
+        for p in range(8):
+            for q in range(p, 8):
+                entry[p][q] = jnp.broadcast_to(column_ref[t, q, p : p + 1, 0:size], shape)
                 entry[q][p] = entry[p][q]
         small = small_inverse(entry)
+        inside = (lane >= k) & (lane < k + 8)
         rows = []
-        for q in range(width):
-            row = jnp.broadcast_to(tiles[t][s + q : s + q + 1, :], shape)
+        for q in range(8):
+            row = jnp.broadcast_to(line_ref[t, q : q + 1, 0:size], shape)
             rows.append(jnp.where(inside, jnp.where(lane == k + q, -1.0, 0.0), row))
-        scaled = []
-        for p in range(width):
-            line = small[p][0] * rows[0]
-            for q in range(1, width):
-                line = line + small[p][q] * rows[q]
-            scaled.append(line)
+        scaled = [added([small[p][q] * rows[q] for q in range(8)]) for p in range(8)]
         fresh = []
-        for r in range(size // 8):
+        for r in range(steps):
+            columns = own if r == t else [column(tiles[r], k + p) for p in range(8)]
             value = jnp.where(inside, 0.0, tiles[r])
-            for p in range(width):
-                col = own[p] if r == t else jnp.broadcast_to(tiles[r][:, k + p : k + p + 1], shape)
-                value = value - col * scaled[p]
-            fresh.append(value)
-        for p in range(width):
-            fresh[t] = jnp.where(sub == s + p, scaled[p], fresh[t])
+            fresh.append(value - added([columns[p] * scaled[p] for p in range(8)]))
+        for p in range(8):
+            fresh[t] = jnp.where(sub == p, scaled[p], fresh[t])
         tiles = fresh
     return -jnp.concatenate(tiles, axis=0)
 
@@ -98,8 +108,8 @@
 def solve_kernel(
     axes, n, points_hbm, modes_ref, rest, pair, wide_ref, coef_ref, inverse_ref, stat_ref,
     points_ref, index_ref, fit, turned, picked, acc1, acc2, squares,
-    part1, landed1, own1, full1, part2, landed2, own2, full2, part3, landed3, own3, full3,
-    listed, fit_in, rest_in, send1, recv1, share1, gather1, send2, recv2, share2, gather2, send3, recv3, share3, gather3,
+    part1, landed1, own1, full1, part2, mate2, landed2, own2, full2, part3, mate3, landed3, part4, mate4, landed4, own3, full3, line_ref, column_ref,
+    listed, fit_in, rest_in, sems,
 ):
     me = flat_index(axes)
     rows_dev, cols = modes_ref.shape
@@ -111,6 +121,13 @@
     count, first, stride = reducers_of(n, split // 8)
     deep = split // count
     mine = (me - first) // stride
+    pairs = n // 2
+    side = lax.rem(me, 2)
+    partner = me + 1 - 2 * side
+    (send1, recv1, share1, gather1, send2, recv2, share2, gather2, send3, recv3, send4, recv4, share3, gather3) = [
+        sems.at[i] for i in range(14)
+    ]
+    swaps = [(sems.at[14 + 2 * i], sems.at[15 + 2 * i]) for i in range(3)]
     reduces = (me >= first) & (me < first + count * stride) & (lax.rem(me - first + n, stride) == 0)
 
     def fetch_fit(c):
@@ -139,8 +156,6 @@
         pl.semaphore_signal(barrier, inc=1, device_id=peer, device_id_type=LOGICAL)
 
     loop(greet, 1, n)
-    for c in range(chunks):
-        fetch_rest(c).start()
     fit[rows_dev:, :] = jnp.zeros((8, split), F32)
     rest[rows_dev:, :] = jnp.zeros((8, split), F32)
     for total in (acc1, acc2, squares):
@@ -197,35 +212,82 @@
 
     def scatter(part, landed, sent, got):
         def body(off):
-            i = lax.rem(me + off, count)
+            i = lax.rem(me + 3 * off, count)
             peer = first + i * stride
 
             @pl.when(peer != me)
             def _():
                 peer_copy(part.at[i], landed.at[me], sent, got, peer).start()
 
-        loop(body, 0, count)
-
-    def reduce(pieces, own, full, shared, gathered):
+        loop(body, 0, count, UNROLL)
+
+    def fill(part, value):
+        for i in range(count):
+            part[i % 2, i // 2, 0:deep, :] = value[i * deep : (i + 1) * deep, :]
+
+    def swap(part, mate, sems_of):
+        return peer_copy(part.at[1 - side], mate, *sems_of, partner)
+
+    def scatter_pair(part, mate, landed, sems_of, sent, got):
+        swap(part, mate, sems_of).wait_recv()
+        part[side] = part[side] + mate[...]
+
+        def body(off):
+            i = lax.rem(me // 2 + off, count // 2)
+            peer = first + (2 * i + side) * stride
+
+            @pl.when(peer != me)
+            def _():
+                peer_copy(part.at[side, i], landed.at[me // 2], sent, got, peer).start()
+
+        loop(body, 0, count // 2, UNROLL)
+
+    local_pair = reduces & (lax.rem(mine + 2 * n, 2) == side)
+    other_pair = reduces & (lax.rem(mine + 2 * n, 2) != side)
+
+    def share(own, full, shared, gathered):
+        full[mine] = own[...]
+
+        def body(off):
+            ahead = off + n // 4 - 1
+            peer = lax.rem(me + jnp.where(ahead < n, ahead, ahead - n + 1), n)
+            peer_copy(own, full.at[mine], shared, gathered, peer).start()
+
+        loop(body, 1, n, UNROLL)
+
+    def summed(landed):
+        return added([landed[j] for j in range(landed.shape[0])])
+
+    def reduce_all(part, landed, own, full, got, shared, gathered):
+        @pl.when(reduces)
+        def _():
+            seen = landed.at[pl.ds(0, n - 1)]
+            peer_copy(seen, seen, shared, got, me).wait_recv()
+            landed[me] = part[mine]
+            own[...] = summed(landed)
+            share(own, full, shared, gathered)
+
+    def reduce_pairs(pieces, own, full, shared, gathered):
+        @pl.when(local_pair)
+        def _():
+            for part, landed, got in pieces:
+                seen = landed.at[pl.ds(0, pairs - 1)]
+                peer_copy(seen, seen, shared, got, me).wait_recv()
+                landed[me // 2] = part[side, mine // 2]
+
+        @pl.when(other_pair)
+        def _():
+            for part, landed, got in pieces:
+                seen = landed.at[pl.ds(0, pairs)]
+                peer_copy(seen, seen, shared, got, me).wait_recv()
+
         @pl.when(reduces)
         def _():
             at = 0
             for part, landed, got in pieces:
-                seen = landed.at[pl.ds(0, n - 1)]
-                peer_copy(seen, seen, shared, got, me).wait_recv()
-                landed[me] = part[mine]
-                total = landed[0]
-                for j in range(1, n):
-                    total = total + landed[j]
-                own[at : at + total.shape[0], :] = total
-                at += total.shape[0]
-            full[mine] = own[...]
-
-            def body(off):
-                peer = lax.rem(me + off, n)
-                peer_copy(own, full.at[mine], shared, gathered, peer).start()
-
-            loop(body, 1, n)
+                own[at : at + landed.shape[1], :] = summed(landed)
+                at += landed.shape[1]
+            share(own, full, shared, gathered)
 
     def collect(full, shared, gathered):
         for held_here, size in ((reduces, count - 1), (jnp.logical_not(reduces), count)):
@@ -235,15 +297,7 @@
                 seen = full.at[pl.ds(0, size)]
                 peer_copy(seen, seen, shared, gathered, me).wait_recv()
 
-    def drain(parts, full, shared):
-        for held_here, size in ((reduces, count - 1), (jnp.logical_not(reduces), count)):
-
-            @pl.when(held_here)
-            def _():
-                for part, sent in parts:
-                    seen = part.at[pl.ds(0, size)]
-                    peer_copy(seen, seen, sent, shared, me).wait_send()
-
+    def drain_shared(full, shared):
         @pl.when(reduces)
         def _():
             seen = full.at[pl.ds(0, count)]
@@ -252,11 +306,23 @@
             rest_of = full.at[pl.ds(0, (n - 1) % count)]
             peer_copy(rest_of, rest_of, shared, shared, me).wait_send()
 
+    def drain_sent(pieces, skips, size):
+        for held_here, some in ((skips, size - 1), (jnp.logical_not(skips), size)):
+
+            @pl.when(held_here)
+            def _():
+                for part, sent in pieces:
+                    seen = part.at[pl.ds(0, some)]
+                    peer_copy(seen, seen, sent, sent, me).wait_send()
+
     waves = chunks // wave
     with jax.named_scope("fgram"):
         for c in range(waves):
             for i in range(wave):
                 fetch_fit(c * wave + i).wait()
+            if c == max(waves - 3, 0):
+                for i in range(chunks):
+                    fetch_rest(i).start()
             if c < waves - 1:
                 fit_gram(c)
     with jax.named_scope("fpick"):
@@ -271,49 +337,68 @@
 
     with jax.named_scope("fgram2"):
         fit_gram(waves - 1)
+        total = acc1[0] + acc1[1]
+        cross = total[:, split:]
+        fill(part2, total[:, :split] + (cross + cross.T))
+        swap(part2, mate2, swaps[0]).start()
     for c in range(waves):
         with jax.named_scope("rgram"):
             rest_gram(c)
-        if c == 0:
+        if c == SEND_FIT:
             with jax.named_scope("scat2"):
-                total = acc1[0] + acc1[1]
-                cross = total[:, split:]
-                part2[...] = (total[:, :split] + (cross + cross.T)).reshape(part2.shape)
-                scatter(part2, landed2, send2, recv2)
+                scatter_pair(part2, mate2, landed2, swaps[0], send2, recv2)
+    with jax.named_scope("swap3"):
+        total = acc2[0] + acc2[1]
+        fill(part3, total[:split, :split] + (total[:split, split:] + total[split:, :split]))
+        swap(part3, mate3, swaps[1]).start()
     with jax.named_scope("rpick"):
         take(rest, 1)
     with jax.named_scope("rdot"):
-        cross = dot(picked[0].reshape(padded, split), picked[1].reshape(padded, split), ((0,), (0,)))
-        total = acc2[0] + acc2[1]
-        ftr = total[:split, :split] + (total[:split, split:] + total[split:, :split])
         fresh = npts - PRIOR - 1
-        tail = slice(2 * deep, 2 * deep + 1)
-        part3[:, tail, :] = jnp.zeros((count, 1, split), F32)
-        part3[:, 0:deep, :] = cross.reshape(count, deep, split)
-        part3[:, deep : 2 * deep, :] = ftr.reshape(count, deep, split)
+        tail = slice(deep, deep + 1)
+        part4[:, :, tail, :] = jnp.zeros((2, count // 2, 1, split), F32)
+        fill(part4, dot(picked[0].reshape(padded, split), picked[1].reshape(padded, split), ((0,), (0,))))
         for i in range(fresh):
-            for half in range(2):
+            for side_of in range(2):
                 at = PRIOR + 1 + i
-                part3[2 * i + half, tail, :] = picked[half, at // 8, at % 8 : at % 8 + 1, :]
-        part3[2 * fresh, tail, :] = jnp.sum(squares[...], axis=0, keepdims=True)
+                part4[side_of, i, tail, :] = picked[side_of, at // 8, at % 8 : at % 8 + 1, :]
+        part4[0, fresh, tail, :] = jnp.sum(squares[...], axis=0, keepdims=True)
+        swap(part4, mate4, swaps[2]).start()
     with jax.named_scope("scat3"):
-        scatter(part3, landed3, send3, recv3)
+        scatter_pair(part3, mate3, landed3, swaps[1], send3, recv3)
+    with jax.named_scope("scat4"):
+        scatter_pair(part4, mate4, landed4, swaps[2], send4, recv4)
 
     with jax.named_scope("red1"):
-        reduce([(part1, landed1, recv1)], own1, full1, share1, gather1)
+        reduce_all(part1, landed1, own1, full1, recv1, share1, gather1)
     with jax.named_scope("col1"):
         collect(full1, share1, gather1)
 
+    half = split // 2
+
     def hook(k):
+        if k == HOOK_REST:
+            with jax.named_scope("red3"):
+                reduce_pairs([(part4, landed4, recv4)], own3, full3, share3, gather3)
         if k == HOOK_FIT:
             with jax.named_scope("red2"):
-                reduce([(part2, landed2, recv2)], own2, full2, share2, gather2)
-        if k == HOOK_REST:
-            with jax.named_scope("red3"):
-                reduce([(part3, landed3, recv3)], own3, full3, share3, gather3)
-
-    with jax.named_scope("sweep"):
-        inverse = sweep_inverse(full1[...].reshape(split, split), hook)
+                reduce_pairs([(part2, landed2, recv2), (part3, landed3, recv3)], own2, full2, share2, gather2)
+
+    with jax.named_scope("sweepP"):
+        gram = full1[...].reshape(split, split)
+        upper = sweep_inverse(gram[:half, :half], hook, line_ref, column_ref)
+    with jax.named_scope("mid"):
+        corner = gram[:half, half:]
+        link = dot(upper, corner)
+        schur = gram[half:, half:] - dot(corner, link, ((0,), (0,)))
+    with jax.named_scope("sweepZ"):
+        later = pl.ds(half // 8, half // 8)
+        lower = sweep_inverse(schur, lambda k: None, line_ref.at[later], column_ref.at[later])
+    with jax.named_scope("join"):
+        bridge = dot(link, lower)
+        above = jnp.concatenate([upper + dot(bridge, link, ((1,), (1,))), -bridge], axis=1)
+        inverse = jnp.concatenate([above, jnp.concatenate([-bridge.T, lower], axis=1)], axis=0)
+        inverse_ref[...] = inverse
     with jax.named_scope("col3"):
         collect(full3, share3, gather3)
     with jax.named_scope("coef"):
@@ -324,21 +409,23 @@
         wide_ref[0:split, split:] = c_lo
         wide_ref[split:, split:] = jnp.zeros((split, split), BF16)
         coef_ref[...] = coef
-        inverse_ref[...] = inverse
-        stat_ref[0:split, split:] = full3[:, deep : 2 * deep, :].reshape(split, split)
         zero = jnp.zeros((8 - fresh, split), F32)
-        for half in range(2):
-            lines = [full3[2 * i + half, tail, :] for i in range(fresh)]
-            stat_ref[split : split + 8, half * split : (half + 1) * split] = jnp.concatenate(lines + [zero], axis=0)
+        for part in range(2):
+            lines = [full3[2 * i + part, tail, :] for i in range(fresh)]
+            stat_ref[split : split + 8, part * split : (part + 1) * split] = jnp.concatenate(lines + [zero], axis=0)
         stat_ref[split + 8 :, 0:split] = jnp.broadcast_to(full3[2 * fresh, tail, :], (8, split))
         stat_ref[split + 8 :, split:] = jnp.zeros((8, split), F32)
     with jax.named_scope("col2"):
         collect(full2, share2, gather2)
-        stat_ref[0:split, 0:split] = full2[...].reshape(split, split)
+        stat_ref[0:split, 0:split] = full2[:, 0:deep, :].reshape(split, split)
+        stat_ref[0:split, split:] = full2[:, deep:, :].reshape(split, split)
     with jax.named_scope("drain"):
-        drain([(part1, send1)], full1, share1)
-        drain([(part2, send2)], full2, share2)
-        drain([(part3, send3)], full3, share3)
+        drain_sent([(part1, send1)], reduces, count)
+        drain_sent([(mate2, send2), (mate3, send3), (mate4, send4)], local_pair, count // 2)
+        for part, mate, sems_of in ((part2, mate2, swaps[0]), (part3, mate3, swaps[1]), (part4, mate4, swaps[2])):
+            swap(part, mate, sems_of).wait_send()
+        for full, shared in ((full1, share1), (full2, share2), (full3, share3)):
+            drain_shared(full, shared)
 
 
 def residual_kernel(
@@ -352,21 +439,15 @@
     def flush(c):
         return pltpu.make_async_copy(made_buf.at[c], res_ref.at[pl.ds(c * rows, rows), :], wrote.at[c])
 
-    wide = wide_ref[...]
-    for c in range(chunks):
-        for at in range(0, rows, piece):
-            here = slice(c * rows + at, c * rows + at + piece)
-            made = jnp.dot(pair[here, :], wide, preferred_element_type=F32)
-            made_buf[c, at : at + piece, :] = rest[here, :] - (made[:, :split] + made[:, split:])
-        flush(c).start()
-    with jax.named_scope("chain"):
+    norm_copy = pltpu.make_async_copy(norm_buf, norm_ref, normed)
+
+    def tail():
         coef = coef_ref[...]
         lefts = stat_ref[split : split + 8, 0:split]
         gains = dot(lefts, inverse_ref[...])
         errors = stat_ref[split : split + 8, split:] - dot(lefts, coef)
-        kept = [coef]
+        yield
         done = []
-        pad7 = jnp.zeros((7, split), F32)
         for j in reversed(range(fresh)):
             left = lefts[j : j + 1, :]
             k = gains[j : j + 1, :]
@@ -378,18 +459,34 @@
             s = 1.0 - jnp.sum(k * left, axis=1, keepdims=True)
             d = d / s
             done.append((k, s, d))
+            yield
+        pad7 = jnp.zeros((7, split), F32)
+        kept = [coef]
+        for k, _, d in done:
             turn = dot(jnp.concatenate([k, pad7], axis=0), jnp.concatenate([d, pad7], axis=0), ((0,), (0,)))
             kept.append(kept[-1] - turn)
         kept = kept[::-1]
-    with jax.named_scope("curved"):
+        yield
         ftf, ftr = stat_ref[0:split, 0:split], stat_ref[0:split, split:]
         sq = stat_ref[split + 8 : split + 9, 0:split]
         curved = dot(ftf, jnp.concatenate(kept, axis=1))
+        yield
         for j in range(steps):
             bent = kept[j] * (curved[:, j * split : (j + 1) * split] - 2.0 * ftr)
             norm_buf[j : j + 1, :] = (sq + jnp.sum(bent, axis=0, keepdims=True)) / total_rows
-    norm_copy = pltpu.make_async_copy(norm_buf, norm_ref, normed)
-    norm_copy.start()
+        norm_copy.start()
+
+    stages = tail()
+    wide = wide_ref[...]
+    for c in range(chunks):
+        for at in range(0, rows, piece):
+            here = slice(c * rows + at, c * rows + at + piece)
+            made = jnp.dot(pair[here, :], wide, preferred_element_type=F32)
+            made_buf[c, at : at + piece, :] = rest[here, :] - (made[:, :split] + made[:, split:])
+        next(stages, None)
+        flush(c).start()
+    for _ in stages:
+        pass
     with jax.named_scope("flushwait"):
         for c in range(chunks):
             flush(c).wait()
@@ -411,6 +508,13 @@
 
     def sources(depth):
         return [pltpu.VMEM((count, depth, split), F32), pltpu.VMEM((n, depth, split), F32)]
+
+    def paired(depth):
+        return [
+            pltpu.VMEM((2, count // 2, depth, split), F32),
+            pltpu.VMEM((count // 2, depth, split), F32),
+            pltpu.VMEM((n // 2, depth, split), F32),
+        ]
 
     def sums(depth):
         return [pltpu.VMEM((depth, split), F32), pltpu.VMEM((count, depth, split), F32)]
@@ -440,13 +544,15 @@
         ]
         + sources(deep)
         + sums(deep)
-        + sources(deep)
-        + sums(deep)
-        + sources(2 * deep + 1)
-        + sums(2 * deep + 1)
+        + paired(deep)
+        + sums(2 * deep)
+        + paired(deep)
+        + paired(deep + 1)
+        + sums(deep + 1)
+        + [pltpu.VMEM((split // 8, 8, split), F32), pltpu.VMEM((split // 8, 8, 8, split), F32)]
         + [pltpu.SemaphoreType.DMA]
         + [pltpu.SemaphoreType.DMA((in_chunks,))] * 2
-        + [pltpu.SemaphoreType.DMA] * 12,
+        + [pltpu.SemaphoreType.DMA((20,))],
         compiler_params=pltpu.CompilerParams(
             collective_id=0, has_side_effects=True, vmem_limit_bytes=24 * 1024 * 1024
         ),

time: 28 us -> 27.1 us (0.968)
  Pallas kernels: 27.2 us -> 26.4 us
    pallas_call x1, Pallas kernels: 23.8 us -> 22.9 us  [on_device(): pl.pallas_call(functools.partial(solve_kernel, axes, n), out_shape=[pltpu...]
where the time goes in v4:
time: 27.1 us; the launch traced here: 27 us
  Pallas kernels  26.4 us (97%)
  between operations  0.64 us (2%)
    pallas_call x1, Pallas kernels, on_device(): pl.pallas_call(functools.partial(solve_kernel, axes, n), out_shape=[pltpu...  22.9 us
    pallas_call x1, Pallas kernels, on_device(): pl.pallas_call(functools.partial(residual_kernel, rows_dev * n), out_shap...  3.44 us

profile of v4, /device:TPU:0, one launch (start us, length us, event | category | flops | bytes accessed | tf_op | source)
XLA Modules:
  0.0 27.0 jit_solution(15026005898898571159)
XLA Ops:
  0.6 22.9 %solve.1 = (f32[12296,128]{1,0:T(8,128)S(1)}, bf16[12288,256]{1,0:T(8,128)(2,1)S(1)}, bf16[256,256]{1,0:T(8,128)(2,1)S(1)}, f32[128,128]{1,0:T(8,128)S(1)}, f32[...) custom-call(s32[196]{0:T(256)} %points_hbm.1, f32[12288,256]{1,0:T(8,128)} %modes_ref.1), custom_call_target="tpu_custom_call" | custom-call | tf_op jit(solution)/shard_map/solve/pallas_call | solution.py:523
  23.6 3.4 %residual.1 = (f32[12288,128]{1,0:T(8,128)}, f32[4,128]{1,0:T(4,128)}) custom-call(f32[12296,128]{1,0:T(8,128)S(1)} %get-tuple-element.8.rest, bf16[12288,256]{1,0:T(8,128)(2,1)S(1)} %get-tuple-element.9.pair, bf16[256,256]{1,0:T(8,128)(2,1)S(1)} %get-tuple-element.10.wide_ref, f32[128,128]{1,0:T(8,128)S(1)} %get-tuple-element.11.coef_ref, ...), custom_call_target="tpu_custom_call" | custom-call | tf_op jit(solution)/shard_map/residual/pallas_call | solution.py:561

commit v5 on v4

--- a/solution.py
+++ b/solution.py
@@ -8,10 +8,10 @@
 from jax.sharding import PartitionSpec as P
 
 PRIOR = 192
-HOOK_REST, HOOK_FIT = 8, 24
+HOOK_REST, HOOK_FIT = 0, 8
 WAVE = 1
 UNROLL = 8
-SEND_FIT = 3
+SEND_FIT = 2
 HIGH = lax.Precision.HIGHEST
 LOGICAL = pl.DeviceIdType.LOGICAL
 F32 = jnp.float32
@@ -108,7 +108,7 @@
 def solve_kernel(
     axes, n, points_hbm, modes_ref, rest, pair, wide_ref, coef_ref, inverse_ref, stat_ref,
     points_ref, index_ref, fit, turned, picked, acc1, acc2, squares,
-    part1, landed1, own1, full1, part2, mate2, landed2, own2, full2, part3, mate3, landed3, part4, mate4, landed4, own3, full3, line_ref, column_ref,
+    part1, landed1, own1, full1, part2, mate2, landed2, own2, full2, part3, mate3, landed3, part4, mate4, landed4, own3, full3, own4, full4, line_ref, column_ref,
     listed, fit_in, rest_in, sems,
 ):
     me = flat_index(axes)
@@ -124,10 +124,10 @@
     pairs = n // 2
     side = lax.rem(me, 2)
     partner = me + 1 - 2 * side
-    (send1, recv1, share1, gather1, send2, recv2, share2, gather2, send3, recv3, send4, recv4, share3, gather3) = [
-        sems.at[i] for i in range(14)
+    (send1, recv1, share1, gather1, send2, recv2, share2, gather2, send3, recv3, send4, recv4, share3, gather3, share4, gather4) = [
+        sems.at[i] for i in range(16)
     ]
-    swaps = [(sems.at[14 + 2 * i], sems.at[15 + 2 * i]) for i in range(3)]
+    swaps = [(sems.at[16 + 2 * i], sems.at[17 + 2 * i]) for i in range(3)]
     reduces = (me >= first) & (me < first + count * stride) & (lax.rem(me - first + n, stride) == 0)
 
     def fetch_fit(c):
@@ -371,6 +371,8 @@
 
     with jax.named_scope("red1"):
         reduce_all(part1, landed1, own1, full1, recv1, share1, gather1)
+    with jax.named_scope("red2"):
+        reduce_pairs([(part2, landed2, recv2)], own2, full2, share2, gather2)
     with jax.named_scope("col1"):
         collect(full1, share1, gather1)
 
@@ -381,8 +383,8 @@
             with jax.named_scope("red3"):
                 reduce_pairs([(part4, landed4, recv4)], own3, full3, share3, gather3)
         if k == HOOK_FIT:
-            with jax.named_scope("red2"):
-                reduce_pairs([(part2, landed2, recv2), (part3, landed3, recv3)], own2, full2, share2, gather2)
+            with jax.named_scope("red4"):
+                reduce_pairs([(part3, landed3, recv3)], own4, full4, share4, gather4)
 
     with jax.named_scope("sweepP"):
         gram = full1[...].reshape(split, split)
@@ -417,14 +419,15 @@
         stat_ref[split + 8 :, split:] = jnp.zeros((8, split), F32)
     with jax.named_scope("col2"):
         collect(full2, share2, gather2)
-        stat_ref[0:split, 0:split] = full2[:, 0:deep, :].reshape(split, split)
-        stat_ref[0:split, split:] = full2[:, deep:, :].reshape(split, split)
+        stat_ref[0:split, 0:split] = full2[...].reshape(split, split)
+        collect(full4, share4, gather4)
+        stat_ref[0:split, split:] = full4[...].reshape(split, split)
     with jax.named_scope("drain"):
         drain_sent([(part1, send1)], reduces, count)
         drain_sent([(mate2, send2), (mate3, send3), (mate4, send4)], local_pair, count // 2)
         for part, mate, sems_of in ((part2, mate2, swaps[0]), (part3, mate3, swaps[1]), (part4, mate4, swaps[2])):
             swap(part, mate, sems_of).wait_send()
-        for full, shared in ((full1, share1), (full2, share2), (full3, share3)):
+        for full, shared in ((full1, share1), (full2, share2), (full3, share3), (full4, share4)):
             drain_shared(full, shared)
 
 
@@ -545,14 +548,15 @@
         + sources(deep)
         + sums(deep)
         + paired(deep)
-        + sums(2 * deep)
+        + sums(deep)
         + paired(deep)
         + paired(deep + 1)
         + sums(deep + 1)
+        + sums(deep)
         + [pltpu.VMEM((split // 8, 8, split), F32), pltpu.VMEM((split // 8, 8, 8, split), F32)]
         + [pltpu.SemaphoreType.DMA]
         + [pltpu.SemaphoreType.DMA((in_chunks,))] * 2
-        + [pltpu.SemaphoreType.DMA((20,))],
+        + [pltpu.SemaphoreType.DMA((22,))],
         compiler_params=pltpu.CompilerParams(
             collective_id=0, has_side_effects=True, vmem_limit_bytes=24 * 1024 * 1024
         ),

time: 27.1 us -> 26 us (0.959)
  Pallas kernels: 26.4 us -> 25.3 us
    pallas_call x1, Pallas kernels: 22.9 us -> 21.8 us  [on_device(): pl.pallas_call(functools.partial(solve_kernel, axes, n), out_shape=[pltpu...]
where the time goes in v5:
time: 26 us; the launch traced here: 25.9 us
  Pallas kernels  25.3 us (97%)
  between operations  0.64 us (2%)
    pallas_call x1, Pallas kernels, on_device(): pl.pallas_call(functools.partial(solve_kernel, axes, n), out_shape=[pltpu...  21.8 us
    pallas_call x1, Pallas kernels, on_device(): pl.pallas_call(functools.partial(residual_kernel, rows_dev * n), out_shap...  3.44 us

profile of v5, /device:TPU:0, one launch (start us, length us, event | category | flops | bytes accessed | tf_op | source)
XLA Modules:
  0.0 25.9 jit_solution(1795161560102186753)
XLA Ops:
  0.6 21.8 %solve.1 = (f32[12296,128]{1,0:T(8,128)S(1)}, bf16[12288,256]{1,0:T(8,128)(2,1)S(1)}, bf16[256,256]{1,0:T(8,128)(2,1)S(1)}, f32[128,128]{1,0:T(8,128)S(1)}, f32[...) custom-call(s32[196]{0:T(256)} %points_hbm.1, f32[12288,256]{1,0:T(8,128)} %modes_ref.1), custom_call_target="tpu_custom_call" | custom-call | tf_op jit(solution)/shard_map/solve/pallas_call | solution.py:526
  22.5 3.4 %residual.1 = (f32[12288,128]{1,0:T(8,128)}, f32[4,128]{1,0:T(4,128)}) custom-call(f32[12296,128]{1,0:T(8,128)S(1)} %get-tuple-element.8.rest, bf16[12288,256]{1,0:T(8,128)(2,1)S(1)} %get-tuple-element.9.pair, bf16[256,256]{1,0:T(8,128)(2,1)S(1)} %get-tuple-element.10.wide_ref, f32[128,128]{1,0:T(8,128)S(1)} %get-tuple-element.11.coef_ref, ...), custom_call_target="tpu_custom_call" | custom-call | tf_op jit(solution)/shard_map/residual/pallas_call | solution.py:565

commit v6 on v5

--- a/solution.py
+++ b/solution.py
@@ -245,11 +245,11 @@
     local_pair = reduces & (lax.rem(mine + 2 * n, 2) == side)
     other_pair = reduces & (lax.rem(mine + 2 * n, 2) != side)
 
-    def share(own, full, shared, gathered):
+    def share(own, full, shared, gathered, skip=0):
         full[mine] = own[...]
 
         def body(off):
-            ahead = off + n // 4 - 1
+            ahead = off + max(skip, 1)
             peer = lax.rem(me + jnp.where(ahead < n, ahead, ahead - n + 1), n)
             peer_copy(own, full.at[mine], shared, gathered, peer).start()
 
@@ -265,7 +265,7 @@
             peer_copy(seen, seen, shared, got, me).wait_recv()
             landed[me] = part[mine]
             own[...] = summed(landed)
-            share(own, full, shared, gathered)
+            share(own, full, shared, gathered, n // 4 - 1)
 
     def reduce_pairs(pieces, own, full, shared, gathered):
         @pl.when(local_pair)
@@ -507,7 +507,7 @@
     deep = split // count
     vmem = pl.BlockSpec(memory_space=pltpu.VMEM)
     in_chunks = 6 if rows_dev % 96 == 0 else 1
-    out_chunks = 12 if rows_dev % 96 == 0 else 1
+    out_chunks = 6 if rows_dev % 96 == 0 else 1
 
     def sources(depth):
         return [pltpu.VMEM((count, depth, split), F32), pltpu.VMEM((n, depth, split), F32)]

time: 26 us -> 25.9 us (level)
  no operation moved by 1% of the time
where the time goes in v6:
time: 25.9 us; the launch traced here: 25.7 us
  Pallas kernels  25.1 us (97%)
  between operations  0.64 us (2%)
    pallas_call x1, Pallas kernels, on_device(): pl.pallas_call(functools.partial(solve_kernel, axes, n), out_shape=[pltpu...  21.8 us
    pallas_call x1, Pallas kernels, on_device(): pl.pallas_call(functools.partial(residual_kernel, rows_dev * n), out_shap...  3.25 us

profile of v6, /device:TPU:0, one launch (start us, length us, event | category | flops | bytes accessed | tf_op | source)
XLA Modules:
  0.0 25.7 jit_solution(1090327926387350088)
XLA Ops:
  0.6 21.8 %solve.1 = (f32[12296,128]{1,0:T(8,128)S(1)}, bf16[12288,256]{1,0:T(8,128)(2,1)S(1)}, bf16[256,256]{1,0:T(8,128)(2,1)S(1)}, f32[128,128]{1,0:T(8,128)S(1)}, f32[...) custom-call(s32[196]{0:T(256)} %points_hbm.1, f32[12288,256]{1,0:T(8,128)} %modes_ref.1), custom_call_target="tpu_custom_call" | custom-call | tf_op jit(solution)/shard_map/solve/pallas_call | solution.py:526
  22.5 3.3 %residual.1 = (f32[12288,128]{1,0:T(8,128)}, f32[4,128]{1,0:T(4,128)}) custom-call(f32[12296,128]{1,0:T(8,128)S(1)} %get-tuple-element.8.rest, bf16[12288,256]{1,0:T(8,128)(2,1)S(1)} %get-tuple-element.9.pair, bf16[256,256]{1,0:T(8,128)(2,1)S(1)} %get-tuple-element.10.wide_ref, f32[128,128]{1,0:T(8,128)S(1)} %get-tuple-element.11.coef_ref, ...), custom_call_target="tpu_custom_call" | custom-call | tf_op jit(solution)/shard_map/residual/pallas_call | solution.py:565
